TPU v7x, 16 devices: a whole 2x2x2 slice. The times are simulated.
16 devices in a mesh: dp: 4 (over z, y), tp: 4 (over x, core).
Axes of the slice: x: 2, y: 2, z: 2, core: 2. Of those that a mesh axis runs over, the one named last changes fastest.
Arguments:
- x_in: bfloat16 [4096, 3584], P('dp'), parts along dimension 0
- lengths: int32 [4096], P('dp'), parts along dimension 0
- norm_gain: bfloat16 [2, 3584], replicated
- w_q: bfloat16 [2, 3584, 3584], P(None, None, 'tp')
- w_k: bfloat16 [2, 3584, 512], P(None, None, 'tp')
- w_v: bfloat16 [2, 3584, 512], P(None, None, 'tp')
- w_o: bfloat16 [2, 3584, 3584], P(None, 'tp')
- w_gate: bfloat16 [2, 3584, 18944], P(None, None, 'tp')
- w_up: bfloat16 [2, 3584, 18944], P(None, None, 'tp')
- w_down: bfloat16 [2, 18944, 3584], P(None, 'tp')
- k_cache: bfloat16 [2, 4096, 32, 4, 128], P(None, 'dp', None, 'tp'), parts along dimension 1
- v_cache: bfloat16 [2, 4096, 32, 4, 128], P(None, 'dp', None, 'tp'), parts along dimension 1
Outputs:
- output: bfloat16 [4096, 3584], P('dp'), parts along dimension 0
There are 4 independent parts. A program takes and returns all parts, laid end to end along the dimension named above; an argument that names none is the same for every part.
All inputs are finite; a program needn't handle non-finite values.
Results may differ from a plain program's by a relative error of at most 0.0165402.
Values are sent between devices in bfloat16 or wider.
A program may use at most 1.25 GiB of HBM per device.

v0:
```python
import jax
import jax.numpy as jnp
from jax import lax
from jax.sharding import PartitionSpec as P

NORM_EPS = 1e-5
ROPE_BASE = 500000.0


def rms_norm(x_res, gain_row):
    x_f32 = x_res.astype(jnp.float32)
    inv_rms = lax.rsqrt(jnp.mean(x_f32 * x_f32, axis=-1, keepdims=True) + NORM_EPS)
    return (x_f32 * inv_rms * gain_row.astype(jnp.float32)).astype(jnp.bfloat16)


def rope_rotate(head_vecs, positions):
    head_dim = head_vecs.shape[-1]
    half_dim = head_dim // 2
    inv_freq = 1.0 / (ROPE_BASE ** (jnp.arange(0, head_dim, 2).astype(jnp.float32) / head_dim))
    angles = positions.astype(jnp.float32)[:, None] * inv_freq[None, :]
    cos_ang = jnp.cos(angles)[:, None, :]
    sin_ang = jnp.sin(angles)[:, None, :]
    vec_f32 = head_vecs.astype(jnp.float32)
    rot_first = vec_f32[..., :half_dim]
    rot_second = vec_f32[..., half_dim:]
    return jnp.concatenate([rot_first * cos_ang - rot_second * sin_ang, rot_second * cos_ang + rot_first * sin_ang], axis=-1).astype(jnp.bfloat16)


def decode_attention(q_rot, k_rot, v_new, k_layer, v_layer, lengths):
    attn_scale = q_rot.shape[-1] ** -0.5
    seq_len = k_layer.shape[1]
    cache_logits = jnp.einsum('bkgd,bskd->bkgs', q_rot, k_layer, preferred_element_type=jnp.float32) * attn_scale
    valid_mask = jnp.arange(seq_len)[None, :] < lengths[:, None]
    cache_logits = jnp.where(valid_mask[:, None, None, :], cache_logits, -jnp.inf)
    self_logit = jnp.einsum('clhe,cle->clh', q_rot, k_rot, preferred_element_type=jnp.float32) * attn_scale
    row_peak = jnp.maximum(jnp.max(cache_logits, axis=-1), self_logit)
    cache_w = jnp.exp(cache_logits - row_peak[..., None])
    self_w = jnp.exp(self_logit - row_peak)
    prob_denom = jnp.sum(cache_w, axis=-1) + self_w
    cache_p = (cache_w / prob_denom[..., None]).astype(jnp.bfloat16)
    self_p = (self_w / prob_denom).astype(jnp.bfloat16)
    cache_part = jnp.einsum('bkgs,bskd->bkgd', cache_p, v_layer, preferred_element_type=jnp.float32)
    self_part = self_p.astype(jnp.float32)[..., None] * v_new.astype(jnp.float32)[:, :, None, :]
    return (cache_part + self_part).astype(jnp.bfloat16)


def layer_update(x_res, lengths, gain_row, wq_layer, wk_layer, wv_layer, wo_layer, wg_layer, wu_layer, wd_layer, k_layer, v_layer):
    tok_rows = x_res.shape[0]
    head_dim = k_layer.shape[-1]
    kv_local = k_layer.shape[-2]
    normed = rms_norm(x_res, gain_row)
    q_proj = jnp.dot(normed, wq_layer, preferred_element_type=jnp.float32).astype(jnp.bfloat16).reshape(tok_rows, -1, head_dim)
    k_proj = jnp.dot(normed, wk_layer, preferred_element_type=jnp.float32).astype(jnp.bfloat16).reshape(tok_rows, kv_local, head_dim)
    v_new = jnp.dot(normed, wv_layer, preferred_element_type=jnp.float32).astype(jnp.bfloat16).reshape(tok_rows, kv_local, head_dim)
    q_rot = rope_rotate(q_proj, lengths).reshape(tok_rows, kv_local, -1, head_dim)
    k_rot = rope_rotate(k_proj, lengths)
    attn_flat = decode_attention(q_rot, k_rot, v_new, k_layer, v_layer, lengths).reshape(tok_rows, -1)
    gate_act = jnp.dot(normed, wg_layer, preferred_element_type=jnp.float32).astype(jnp.bfloat16)
    up_act = jnp.dot(normed, wu_layer, preferred_element_type=jnp.float32).astype(jnp.bfloat16)
    mlp_hidden = (jax.nn.silu(gate_act.astype(jnp.float32)) * up_act.astype(jnp.float32)).astype(jnp.bfloat16)
    return jnp.dot(attn_flat, wo_layer, preferred_element_type=jnp.float32) + jnp.dot(mlp_hidden, wd_layer, preferred_element_type=jnp.float32)


def solution(mesh):
    tp_size = mesh.shape['tp']
    arg_specs = (P('dp', None), P('dp'), P(), P(None, None, 'tp'), P(None, None, 'tp'), P(None, None, 'tp'), P(None, 'tp', None), P(None, None, 'tp'), P(None, None, 'tp'), P(None, 'tp', None), P(None, 'dp', None, 'tp', None), P(None, 'dp', None, 'tp', None))

    def per_device(x_in, lengths, norm_gain, w_q, w_k, w_v, w_o, w_gate, w_up, w_down, k_cache, v_cache):
        tok_rows, model_width = x_in.shape
        col_width = model_width // tp_size
        col_start = lax.axis_index('tp') * col_width
        x_res = x_in
        for layer_idx in range(norm_gain.shape[0]):
            update = layer_update(x_res, lengths, norm_gain[layer_idx], w_q[layer_idx], w_k[layer_idx], w_v[layer_idx], w_o[layer_idx], w_gate[layer_idx], w_up[layer_idx], w_down[layer_idx], k_cache[layer_idx], v_cache[layer_idx])
            partial_sum = update.astype(jnp.bfloat16)
            received = lax.all_to_all(partial_sum, 'tp', 1, 0, tiled=True)
            reduced = jnp.sum(received.reshape(tp_size, tok_rows, col_width).astype(jnp.float32), axis=0)
            own_cols = lax.dynamic_slice_in_dim(x_res, col_start, col_width, axis=1)
            new_cols = (own_cols.astype(jnp.float32) + reduced).astype(jnp.bfloat16)
            x_res = lax.all_gather(new_cols, 'tp', axis=1, tiled=True)
        return x_res

    return jax.shard_map(per_device, mesh=mesh, in_specs=arg_specs, out_specs=P('dp', None), check_vma=False)
```

profile of v0, /device:TPU:0, one launch (start us, length us, event | category | flops | bytes accessed | tf_op | source)
XLA Modules:
  0.0 818.7 jit_solution(14025452302723353566)
XLA Ops:
  8.5 4.8 fusion.28
  14.0 3.0 multiply_cosine_fusion
  17.0 3.6 fusion.79
  22.9 2.2 copy.96
  25.1 6.3 fusion.77
  31.4 10.2 %fusion.70 = bf16[1024,896]{0,1:T(8,128)(2,1)S(1)} fusion(bf16[2,3584,896]{2,1,0:T(8,128)(2,1)} %param.15, bf16[1024,3584]{1,0:T(8,128)(2,1)S(1)} %bitcast.121, f32[3584]{0:T(1024)S(1)} %get-tuple-element.6, f32[1024]{0:T(1024)S(1)} %add_rsqrt_fusion.1), kind=kOutput, calls=%fused_computation.104 | convolution fusion | flops 6592266240 | bytes 15616000 | tf_op jit(solution)/shard_map/dot_general | solution.py:52
  43.3 3.9 copy.93
  47.2 2.7 copy.92
  49.9 4.5 subtract_convert_fusion.1
  55.8 2.8 multiply_reduce_fusion.1
  58.7 10.8 %fusion.56 = (f32[1024,7]{1,0:T(8,128)S(1)}, f32[1024,7,32]{2,1,0:T(8,128)}) fusion(pred[1024,32]{1,0:T(8,128)(4,1)S(1)} %iota_compare_fusion, bf16[2,1024,32,1,128]{4,2,1,3,0:T(8,128)(2,1)} %bitcast.118, bf16[1024,7,64]{2,1,0:T(8,128)(2,1)} %copy-done, bf16[1024,7,64]{2,1,0:T(8,128)(2,1)S(1)} %get-tuple-element.9), kind=kOutput, calls=%fused_computation.86 | convolution fusion | flops 63071232 | bytes 12382208 | tf_op jit(solution)/shard_map/bkgd,bskd->bkgs/dot_general | solution.py:32
  70.0 15.9 %fusion.58 = f32[1024,7]{1,0:T(8,128)S(1)} fusion(f32[1024,7,32]{2,1,0:T(8,128)} %get-tuple-element.26, f32[1024,7]{1,0:T(8,128)S(1)} %copy.64, pred[1024,32]{1,0:T(8,128)(4,1)S(1)} %iota_compare_fusion), kind=kLoop, calls=%fused_computation.90 | loop fusion | flops 910336 | bytes 1007616 | tf_op jit(solution)/shard_map/reduce_sum | solution.py:39
  88.2 11.4 %add_convert_fusion.4 = bf16[1024,7,128]{2,1,0:T(8,128)(2,1)} fusion(f32[1024,128]{1,0:T(8,128)} %fusion.77, f32[1024,7]{1,0:T(8,128)} %copy.68, bf16[2,1024,32,1,128]{4,2,1,3,0:T(8,128)(2,1)} %bitcast.132, f32[1024,7,32]{2,1,0:T(8,128)} %get-tuple-element.26, f32[1024,7]{1,0:T(8,128)} %copy.66, f32[1024,7]{1,0:T(8,128)} %copy-done.12, ...), kind=kOutput, calls=%fused_computation.80 | convolution fusion | flops 62619648 | bytes 16547840 | tf_op jit(solution)/shard_map/bkgs,bskd->bkgd/dot_general | solution.py:42
  99.6 4.0 copy.69
  103.6 47.3 %fusion.10 = bf16[1024,4736]{1,0:T(8,128)(2,1)} fusion(bf16[2,3584,4736]{2,1,0:T(8,128)(2,1)} %param.19, bf16[1024,3584]{1,0:T(8,128)(2,1)} %param.12, f32[3584]{0:T(1024)S(1)} %get-tuple-element.6, f32[1024]{0:T(1024)S(1)} %add_rsqrt_fusion.1), kind=kOutput, calls=%fused_computation.10 | convolution fusion | flops 34777071616 | bytes 51005440 | tf_op jit(solution)/shard_map/dot_general | solution.py:58
  150.9 43.3 %fusion.8 = bf16[1024,4736]{1,0:T(8,128)(2,1)} fusion(bf16[2,3584,4736]{2,1,0:T(8,128)(2,1)} %param.20, bf16[1024,3584]{1,0:T(8,128)(2,1)S(1)} %bitcast.123, f32[3584]{0:T(1024)S(1)} %get-tuple-element.6, f32[1024]{0:T(1024)S(1)} %add_rsqrt_fusion.1), kind=kOutput, calls=%fused_computation.8 | convolution fusion | flops 34777071616 | bytes 51005440 | tf_op jit(solution)/shard_map/dot_general | solution.py:59
  194.2 9.9 %fusion.150 = bf16[1024,4736]{1,0:T(8,128)(2,1)S(1)} fusion(bf16[1024,4736]{1,0:T(8,128)(2,1)} %fusion.8, bf16[1024,4736]{1,0:T(8,128)(2,1)} %fusion.10), kind=kLoop, calls=%fused_computation.31.clone.clone.2 | loop fusion | flops 38797312 | bytes 29097984 | tf_op jit(solution)/shard_map/dot_general | solution.py:61
  204.2 41.0 %fusion.6 = f32[1024,3584]{1,0:T(8,128)} fusion(bf16[2,4736,3584]{2,1,0:T(8,128)(2,1)} %param.21, bf16[1024,4736]{1,0:T(8,128)(2,1)S(1)} %fusion.150), kind=kOutput, calls=%fused_computation.6 | convolution fusion | flops 34762391552 | bytes 58327040 | tf_op jit(solution)/shard_map/dot_general | solution.py:61
  245.2 13.4 %add_convert_fusion.1 = bf16[1024,3584]{1,0:T(8,128)(2,1)S(1)} fusion(f32[1024,3584]{1,0:T(8,128)} %fusion.6, bf16[1024,896]{0,1:T(8,128)(2,1)S(1)} %bitcast.130, bf16[2,896,3584]{2,1,0:T(8,128)(2,1)} %param.18), kind=kOutput, calls=%fused_computation.45 | convolution fusion | flops 6584008704 | bytes 30277632 | tf_op jit(solution)/shard_map/dot_general | solution.py:61
  258.6 3.6 copy.103
  262.2 5.5 all-to-all-start
  267.8 82.5 %all-to-all-done = bf16[1024,4,896]{2,0,1:T(8,128)(2,1)} async-done(((bf16[1024,4,896]{2,0,1:T(8,128)(2,1)}), bf16[1024,4,896]{2,0,1:T(8,128)(2,1)}, u32[]{:S(2)}, u32[]{:S(2)}) %all-to-all-start) | async-done | bytes 7340064 | tf_op jit(solution)/shard_map/all_to_all | solution.py:76
  350.2 4.6 convert_reduce_fusion.1
  354.8 3.3 add_convert_fusion.7
  358.2 51.6 %all-gather.3.cloned.1.call-done = bf16[1024,3584]{1,0:T(8,128)(2,1)} async-done(((bf16[1024,896]{1,0:T(8,128)(2,1)}), bf16[1024,3584]{1,0:T(8,128)(2,1)}) %all-gather.3.cloned.1.call-update) | async-done | bytes 7340048 | tf_op jit(solution)/shard_map/all_gather | solution.py:80
  409.8 4.7 fusion.31
  415.0 2.5 fusion.81
  419.7 11.4 %fusion.73 = bf16[1024,896]{0,1:T(8,128)(2,1)S(1)} fusion(bf16[2,3584,896]{2,1,0:T(8,128)(2,1)} %param.15, bf16[1024,3584]{1,0:T(8,128)(2,1)} %all-gather.3.cloned.1.call-done, f32[3584]{0:T(1024)S(1)} %copy-done.20, f32[1024]{0:T(1024)S(1)} %add_rsqrt_fusion), kind=kOutput, calls=%fused_computation.105 | convolution fusion | flops 6592266240 | bytes 15616000 | tf_op jit(solution)/shard_map/dot_general | solution.py:52
  432.8 3.9 copy.95
  436.7 2.7 copy.94
  439.4 4.3 subtract_convert_fusion
  443.8 11.0 %fusion.57 = (f32[1024,7]{1,0:T(8,128)}, f32[1024,7,32]{2,1,0:T(8,128)}) fusion(pred[1024,32]{1,0:T(8,128)(4,1)S(1)} %copy-done.8, bf16[2,1024,32,1,128]{4,2,1,3,0:T(8,128)(2,1)} %bitcast.119, bf16[1024,7,64]{2,1,0:T(8,128)(2,1)S(1)} %get-tuple-element.8, bf16[1024,7,64]{2,1,0:T(8,128)(2,1)S(1)} %get-tuple-element.7), kind=kOutput, calls=%fused_computation.87 | convolution fusion | flops 63071232 | bytes 11202560 | tf_op jit(solution)/shard_map/bkgd,bskd->bkgs/dot_general | solution.py:32
  454.8 3.5 multiply_reduce_fusion
  461.2 16.1 %fusion.59 = f32[1024,7]{1,0:T(8,128)S(1)} fusion(f32[1024,7,32]{2,1,0:T(8,128)} %get-tuple-element.28, f32[1024,7]{1,0:T(8,128)S(1)} %copy.75, pred[1024,32]{1,0:T(8,128)(4,1)S(1)} %copy-done.8), kind=kLoop, calls=%fused_computation.91 | loop fusion | flops 910336 | bytes 1007616 | tf_op jit(solution)/shard_map/reduce_sum | solution.py:39
  479.6 5.3 fusion.76
  485.0 11.3 %add_convert_fusion.2 = bf16[1024,7,128]{2,1,0:T(8,128)(2,1)} fusion(f32[1024,128]{1,0:T(8,128)S(1)} %fusion.76, f32[1024,7]{1,0:T(8,128)S(1)} %copy-done.16, bf16[2,1024,32,1,128]{4,2,1,3,0:T(8,128)(2,1)} %bitcast.133, f32[1024,7,32]{2,1,0:T(8,128)S(1)} %copy-done.1, f32[1024,7]{1,0:T(8,128)S(1)} %copy-done.15, f32[1024,7]{1,0:T(8,128)} %copy-done.11, ...), kind=kOutput, calls=%fused_computation.74 | convolution fusion | flops 62619648 | bytes 12279808 | tf_op jit(solution)/shard_map/bkgs,bskd->bkgd/dot_general | solution.py:42
  496.3 4.0 copy.80
  500.3 47.4 %fusion.4 = bf16[1024,4736]{1,0:T(8,128)(2,1)} fusion(bf16[2,3584,4736]{2,1,0:T(8,128)(2,1)} %param.19, bf16[1024,3584]{1,0:T(8,128)(2,1)} %all-gather.3.cloned.1.call-done, f32[3584]{0:T(1024)S(1)} %copy-done.20, f32[1024]{0:T(1024)S(1)} %add_rsqrt_fusion), kind=kOutput, calls=%fused_computation.4 | convolution fusion | flops 34777071616 | bytes 51005440 | tf_op jit(solution)/shard_map/dot_general | solution.py:58
  547.7 43.4 %fusion.2 = bf16[1024,4736]{1,0:T(8,128)(2,1)} fusion(bf16[2,3584,4736]{2,1,0:T(8,128)(2,1)} %param.20, bf16[1024,3584]{1,0:T(8,128)(2,1)S(1)} %bitcast.125, f32[3584]{0:T(1024)S(1)} %copy-done.20, f32[1024]{0:T(1024)S(1)} %add_rsqrt_fusion), kind=kOutput, calls=%fused_computation.2 | convolution fusion | flops 34777071616 | bytes 51005440 | tf_op jit(solution)/shard_map/dot_general | solution.py:59
  591.1 9.9 %fusion.148 = bf16[1024,4736]{1,0:T(8,128)(2,1)S(1)} fusion(bf16[1024,4736]{1,0:T(8,128)(2,1)} %fusion.2, bf16[1024,4736]{1,0:T(8,128)(2,1)} %fusion.4), kind=kLoop, calls=%fused_computation.30.clone.clone.2 | loop fusion | flops 38797312 | bytes 29097984 | tf_op jit(solution)/shard_map/dot_general | solution.py:61
  601.0 41.0 %fusion = f32[1024,3584]{1,0:T(8,128)} fusion(bf16[2,4736,3584]{2,1,0:T(8,128)(2,1)} %param.21, bf16[1024,4736]{1,0:T(8,128)(2,1)S(1)} %fusion.148), kind=kOutput, calls=%fused_computation | convolution fusion | flops 34762391552 | bytes 58327040 | tf_op jit(solution)/shard_map/dot_general | solution.py:61
  642.0 15.1 %add_convert_fusion = bf16[1024,3584]{1,0:T(8,128)(2,1)} fusion(f32[1024,3584]{1,0:T(8,128)} %fusion, bf16[1024,896]{0,1:T(8,128)(2,1)S(1)} %bitcast.131, bf16[2,896,3584]{2,1,0:T(8,128)(2,1)} %param.18), kind=kOutput, calls=%fused_computation.43 | convolution fusion | flops 6584008704 | bytes 30277632 | tf_op jit(solution)/shard_map/dot_general | solution.py:61
  657.1 3.7 copy.102
  660.8 85.4 %all_to_all.26 = bf16[1024,4,896]{2,0,1:T(8,128)(2,1)} all-to-all(bf16[1024,4,896]{2,0,1:T(8,128)(2,1)S(1)} %bitcast.117), channel_id=1, replica_groups=mesh['dp'=4,'tp'=4] {'tp'}, dimensions={1} | all-to-all | bytes 14680064 | tf_op jit(solution)/shard_map/all_to_all | solution.py:76
  746.3 4.6 convert_reduce_fusion
  750.8 3.2 add_convert_fusion.6
  754.1 50.7 %all-gather.5.cloned.1.call-done = bf16[1024,3584]{1,0:T(8,128)(2,1)} async-done(((bf16[1024,896]{1,0:T(8,128)(2,1)}), bf16[1024,3584]{1,0:T(8,128)(2,1)}) %all-gather.5.cloned.1.call-update) | async-done | bytes 7340048 | tf_op jit(solution)/shard_map/all_gather | solution.py:80
  804.7 6.6 copy.105
  (98 shorter events, 20.3 us)
Async XLA Ops:
  6.5 10.5 %copy-start.2 = (bf16[1024,3584]{1,0:T(8,128)(2,1)S(1)}, bf16[1024,3584]{1,0:T(8,128)(2,1)}, u32[]{:S(2)}) copy-start(bf16[1024,3584]{1,0:T(8,128)(2,1)} %param.12) | copy-start | bytes 22020100
  6.5 6.8 copy-start.19
  6.5 14.1 %copy-start.21 = (f32[64]{0:T(128)}, f32[64]{0:T(128)S(1)}, u32[]{:S(2)}) copy-start(f32[64]{0:T(128)S(1)} %negate_power_fusion) | copy-start | bytes 772
  7.4 13.3 %copy-start.17 = (f32[1024]{0:T(1024)}, f32[1024]{0:T(1024)S(1)}, u32[]{:S(2)}) copy-start(f32[1024]{0:T(1024)S(1)} %convert_element_type.194) | copy-start | bytes 12292
  8.4 79.8 %copy-start.7 = (pred[1024,32]{1,0:T(8,128)(4,1)}, pred[1024,32]{1,0:T(8,128)(4,1)S(1)}, u32[]{:S(2)}) copy-start(pred[1024,32]{1,0:T(8,128)(4,1)S(1)} %iota_compare_fusion) | copy-start | bytes 98308
  22.9 8.5 %slice-start = ((s8[7340032]{0:T(1024)(128)(4,1)}), s8[3145728]{0:T(1024)(128)(4,1)S(1)}, s32[]{:S(2)}) async-start(s8[7340032]{0:T(1024)(128)(4,1)} %bitcast.120), calls=%async_computation.4 | async-start | bytes 6291456
  25.1 6.3 slice-start.1
  43.3 6.6 copy-start.4
  43.3 6.6 copy-start.6
  49.9 5.8 copy-start.10
  54.4 1.3 copy-start
  70.0 18.2 %copy-start.12 = (f32[1024,7]{1,0:T(8,128)}, f32[1024,7]{1,0:T(8,128)S(1)}, u32[]{:S(2)}) copy-start(f32[1024,7]{1,0:T(8,128)S(1)} %copy.64) | copy-start | bytes 86020
  88.2 62.7 %slice-start.2 = ((s8[7340032]{0:T(1024)(128)(4,1)}), s8[3145728]{0:T(1024)(128)(4,1)S(1)}, s32[]{:S(2)}) async-start(s8[7340032]{0:T(1024)(128)(4,1)} %bitcast.122), calls=%async_computation.6 | async-start | bytes 6291456
  103.6 47.3 %slice-start.3 = ((s8[7340032]{0:T(1024)(128)(4,1)}), s8[4194304]{0:T(1024)(128)(4,1)S(1)}, s32[]{:S(2)}) async-start(s8[7340032]{0:T(1024)(128)(4,1)} %bitcast.122), calls=%async_computation.7 | async-start | bytes 8388608
  204.1 41.1 %copy-start.13 = (bf16[1024,7,128]{0,2,1:T(8,128)(2,1)S(1)}, bf16[1024,7,128]{0,2,1:T(8,128)(2,1)}, u32[]{:S(2)}) copy-start(bf16[1024,7,128]{0,2,1:T(8,128)(2,1)} %copy.69) | copy-start | bytes 5505028
  262.2 88.0 %all-to-all-start = ((bf16[1024,4,896]{2,0,1:T(8,128)(2,1)}), bf16[1024,4,896]{2,0,1:T(8,128)(2,1)}, u32[]{:S(2)}, u32[]{:S(2)}) async-start(bf16[1024,4,896]{2,0,1:T(8,128)(2,1)} %bitcast.116), calls=%async_computation | async-start | bytes 14680064 | tf_op jit(solution)/shard_map/all_to_all | solution.py:76
  267.7 142.1 %all-gather.3.cloned.1.call-start = ((), (), s32[]{:S(2)}) async-start(), calls=%async_computation.2 | async-start | bytes 9175040 | tf_op jit(solution)/shard_map/all_gather | solution.py:80
  354.8 59.8 %copy-start.20 = (f32[3584]{0:T(1024)S(1)}, f32[3584]{0:T(1024)}, u32[]{:S(2)}) copy-start(f32[3584]{0:T(1024)} %get-tuple-element.5) | copy-start | bytes 43012
  354.8 59.8 %copy-start.23 = (bf16[2,3584,128]{2,1,0:T(8,128)(2,1)S(1)}, bf16[2,3584,128]{2,1,0:T(8,128)(2,1)}, u32[]{:S(2)}) copy-start(bf16[2,3584,128]{2,1,0:T(8,128)(2,1)} %param.16) | copy-start | bytes 5505028
  358.2 446.6 %all-gather.5.cloned.1.call-start = ((), (), s32[]{:S(2)}) async-start(), calls=%async_computation.3 | async-start | bytes 9175040 | tf_op jit(solution)/shard_map/all_gather | solution.py:80
  409.8 5.2 copy-start.3
  415.0 2.5 copy-start.18
  415.0 2.5 copy-start.22
  432.8 6.6 copy-start.5
  439.4 4.3 copy-start.8
  443.8 11.0 %copy-start.9 = (f32[1024,128]{1,0:T(8,128)S(1)}, f32[1024,128]{1,0:T(8,128)}, u32[]{:S(2)}) copy-start(f32[1024,128]{1,0:T(8,128)} %copy.97) | copy-start | bytes 1572868
  458.3 21.2 %copy-start.24 = (bf16[2,3584,128]{2,1,0:T(8,128)(2,1)S(1)}, bf16[2,3584,128]{2,1,0:T(8,128)(2,1)}, u32[]{:S(2)}) copy-start(bf16[2,3584,128]{2,1,0:T(8,128)(2,1)} %param.17) | copy-start | bytes 5505028
  461.2 18.4 %copy-start.11 = (f32[1024,7]{1,0:T(8,128)}, f32[1024,7]{1,0:T(8,128)S(1)}, u32[]{:S(2)}) copy-start(f32[1024,7]{1,0:T(8,128)S(1)} %copy.75) | copy-start | bytes 86020
  479.6 5.4 copy-start.1
  479.6 5.4 copy-start.15
  479.6 5.4 copy-start.16
  485.0 62.7 %slice-start.4 = ((s8[7340032]{0:T(1024)(128)(4,1)}), s8[3145728]{0:T(1024)(128)(4,1)S(1)}, s32[]{:S(2)}) async-start(s8[7340032]{0:T(1024)(128)(4,1)} %bitcast.124), calls=%async_computation.8 | async-start | bytes 6291456
  500.3 47.4 %slice-start.5 = ((s8[7340032]{0:T(1024)(128)(4,1)}), s8[4194304]{0:T(1024)(128)(4,1)S(1)}, s32[]{:S(2)}) async-start(s8[7340032]{0:T(1024)(128)(4,1)} %bitcast.124), calls=%async_computation.9 | async-start | bytes 8388608
  601.0 41.0 %copy-start.14 = (bf16[1024,7,128]{0,2,1:T(8,128)(2,1)S(1)}, bf16[1024,7,128]{0,2,1:T(8,128)(2,1)}, u32[]{:S(2)}) copy-start(bf16[1024,7,128]{0,2,1:T(8,128)(2,1)} %copy.80) | copy-start | bytes 5505028
Sparse Core Ops, SparseCore 0:
  358.3 51.4 all-gather.2
  754.2 50.5 all-gather.4
where the time goes:
time: 824 us; the launch traced here: 819 us
  matrix products  376 us (46%)
  waiting for transfers between devices  185 us (22%)
  other arithmetic  101 us (12%)
  blocking collectives  85.4 us (10%)
  local copies, waits for them, and re-layouts  51.4 us (6%)
  between operations  14.3 us (2%)
    all_gather x2, waiting for transfers between devices, per_device(): x_res = lax.all_gather(new_cols, 'tp', axis=1, tiled=True)  102 us
    dot_general x2, matrix products, layer_update(): jnp.dot(normed, wg_layer, preferred_element_type=jnp.float32)  94.7 us
    dot_general x2, matrix products, layer_update(): jnp.dot(normed, wu_layer, preferred_element_type=jnp.float32)  86.7 us
    all_to_all x1, blocking collectives, per_device(): received = lax.all_to_all(partial_sum, 'tp', 1, 0, tiled=True)  85.4 us
    all_to_all x1, waiting for transfers between devices, per_device(): received = lax.all_to_all(partial_sum, 'tp', 1, 0, tiled=True)  82.5 us
    dot_general x2, matrix products, layer_update(): jnp.dot(mlp_hidden, wd_layer, preferred_element_type=jnp.float32)  82.1 us
    reduce_sum x2, other arithmetic, decode_attention(): prob_denom = jnp.sum(cache_w, axis=-1) + self_w  32 us
    dot_general x2, matrix products, layer_update(): jnp.dot(attn_flat, wo_layer, preferred_element_type=jnp.float32)  28.5 us
  transfers between devices with their start and end apart: 3, of which 3 were waited for; matrix products, arithmetic and copies ran while one was open for 0% of the time, Pallas kernels for 0%

commit v1 on v0

v1 whole, which is shorter than its diff:
```python
import functools

import jax
import jax.numpy as jnp
from jax import lax
from jax.experimental import pallas as pl
from jax.experimental.pallas import tpu as pltpu
from jax.sharding import PartitionSpec as P

NORM_EPS = 1e-5
ROPE_BASE = 500000.0
MESH = pl.DeviceIdType.MESH
F32 = jnp.float32
BF16 = jnp.bfloat16

CHUNKS = 2
GU_TILE = 512
DN_TILE = 512
SUB = 256
KV_TOK = 64
GRP = 16
ROWS = 16
HOOK_SUM = 5
HOOK_FWD = 2


def layers_kernel(tp, dims, *refs):
    (x_in, lens, cos_t, sin_t, gain, wq, wk, wv, wo, wg, wu, wd, kc, vc, out,
     act, w1, wsp, w2, hid, qk, vnew, kbuf, vbuf, share, recv, xres,
     w1_sem, wsp_sem, w2_sem, kv_sem, io_sem, rs_send, rs_recv, ag_send, ag_recv) = refs
    L, tok, D, QW, HD, FF, SEQ = dims
    M = tok // CHUNKS
    Q = M // tp
    NH = QW // HD
    iters = L * CHUNKS
    GU_N = FF // GU_TILE
    REM = FF - GU_N * GU_TILE
    DN_N = D // DN_TILE
    KV_N = M // KV_TOK

    me = lax.axis_index("tp")
    half = me // 2
    low = me - half * 2
    sib = half * 2 + (1 - low)
    cross = (1 - half) * 2 + low
    diag = (1 - half) * 2 + (1 - low)
    peers = (sib, cross, diag)
    my_rows = pl.ds(pl.multiple_of(me * Q, Q), Q)

    def rows_of(dev):
        return pl.ds(pl.multiple_of(dev * Q, Q), Q)

    def qk_copies(l):
        return [pltpu.make_async_copy(wq.at[l], w1.at[0, :, pl.ds(0, QW)], w1_sem.at[0, 0]),
                pltpu.make_async_copy(wk.at[l], w1.at[0, :, pl.ds(QW, HD)], w1_sem.at[0, 1])]

    def gu_copies(l, j, slot):
        cols = pl.ds(pl.multiple_of(j * GU_TILE, GU_TILE), GU_TILE)
        return [pltpu.make_async_copy(wg.at[l, :, cols], w1.at[slot, :, pl.ds(0, GU_TILE)], w1_sem.at[slot, 0]),
                pltpu.make_async_copy(wu.at[l, :, cols], w1.at[slot, :, pl.ds(GU_TILE, GU_TILE)], w1_sem.at[slot, 1])]

    def sp_copies(l):
        rem = pl.ds(GU_N * GU_TILE, REM)
        return [pltpu.make_async_copy(wv.at[l], wsp.at[:, pl.ds(0, HD)], wsp_sem.at[0]),
                pltpu.make_async_copy(wg.at[l, :, rem], wsp.at[:, pl.ds(HD, REM)], wsp_sem.at[1]),
                pltpu.make_async_copy(wu.at[l, :, rem], wsp.at[:, pl.ds(HD + REM, REM)], wsp_sem.at[2])]

    def dn_copies(l, j, slot):
        cols = pl.ds(pl.multiple_of(j * DN_TILE, DN_TILE), DN_TILE)
        return [pltpu.make_async_copy(wo.at[l, :, cols], w2.at[slot, pl.ds(0, QW)], w2_sem.at[slot, 0]),
                pltpu.make_async_copy(wd.at[l, :, cols], w2.at[slot, pl.ds(QW, FF)], w2_sem.at[slot, 1])]

    def kv_copies(l, c, b, slot):
        toks = pl.ds(pl.multiple_of(c * M + b * KV_TOK, KV_TOK), KV_TOK)
        return [pltpu.make_async_copy(kc.at[l, toks], kbuf.at[slot], kv_sem.at[slot, 0]),
                pltpu.make_async_copy(vc.at[l, toks], vbuf.at[slot], kv_sem.at[slot, 1])]

    def start(copies):
        for cp in copies:
            cp.start()

    def wait(copies):
        for cp in copies:
            cp.wait()

    def share_copy(c, k, j):
        cols = pl.ds(pl.multiple_of(j * DN_TILE, DN_TILE), DN_TILE)
        return pltpu.make_async_remote_copy(
            src_ref=share.at[rows_of(peers[k]), cols], dst_ref=recv.at[c, k, :, cols],
            send_sem=rs_send.at[k], recv_sem=rs_recv.at[c, k],
            device_id={"tp": peers[k]}, device_id_type=MESH)

    def share_all(c, k):
        return pltpu.make_async_remote_copy(
            src_ref=share.at[rows_of(peers[k])], dst_ref=recv.at[c, k],
            send_sem=rs_send.at[k], recv_sem=rs_recv.at[c, k],
            device_id={"tp": peers[k]}, device_id_type=MESH)

    def gather_copy(c, k):
        block = rows_of(cross) if k == 2 else my_rows
        to = cross if k == 1 else sib
        return pltpu.make_async_remote_copy(
            src_ref=act.at[c, block], dst_ref=act.at[c, block],
            send_sem=ag_send.at[c, k], recv_sem=ag_recv.at[c, k],
            device_id={"tp": to}, device_id_type=MESH)

    def normed(xf, grow):
        inv = lax.rsqrt(jnp.mean(xf * xf, axis=-1, keepdims=True) + NORM_EPS)
        return (xf * inv * grow).astype(BF16)

    def sum_and_send(l, c):
        for k in range(3):
            share_all(c, k).wait_recv()
        last = l == L - 1
        grow = gain[jnp.minimum(l + 1, L - 1)]

        def step(r, carry):
            rr = pl.ds(pl.multiple_of(r * ROWS, ROWS), ROWS)
            own = pl.ds(pl.multiple_of(me * Q + r * ROWS, ROWS), ROWS)
            s = share[own, :].astype(F32)
            for k in range(3):
                s = s + recv[c, k, rr, :].astype(F32)
            xn = (xres[c, rr, :].astype(F32) + s).astype(BF16)
            xres[c, rr, :] = xn

            @pl.when(last)
            def _():
                act[c, own, :] = xn

            @pl.when(jnp.logical_not(last))
            def _():
                act[c, own, :] = normed(xn.astype(F32), grow)
            return carry

        lax.fori_loop(0, Q // ROWS, step, 0)
        gather_copy(c, 1).start()
        gather_copy(c, 0).start()

    def forward(c):
        gather_copy(c, 1).wait_recv()
        gather_copy(c, 2).start()

    def gathered(c):
        gather_copy(c, 0).wait_recv()
        gather_copy(c, 2).wait_recv()
        for k in range(3):
            gather_copy(c, k).wait_send()

    x_copies = [pltpu.make_async_copy(x_in.at[pl.ds(c * M, M)], act.at[c], io_sem.at[c]) for c in range(CHUNKS)]
    res_copies = [pltpu.make_async_copy(x_in.at[pl.ds(pl.multiple_of(c * M + me * Q, Q), Q)], xres.at[c], io_sem.at[CHUNKS + c])
                  for c in range(CHUNKS)]
    x_copies[0].start()
    start(qk_copies(0))
    start(sp_copies(0))
    start(kv_copies(0, 0, 0, 0))
    start(x_copies[1:])
    start(res_copies)

    barrier = pltpu.get_barrier_semaphore()
    for p in peers:
        pl.semaphore_signal(barrier, inc=1, device_id={"tp": p}, device_id_type=MESH)
    pl.semaphore_wait(barrier, 3)

    grow0 = gain[0]

    def first_norm(c):
        x_copies[c].wait()

        def step(r, carry):
            rr = pl.ds(pl.multiple_of(r * ROWS, ROWS), ROWS)
            act[c, rr, :] = normed(act[c, rr, :].astype(F32), grow0)
            return carry

        lax.fori_loop(0, M // ROWS, step, 0)

    first_norm(0)
    wait(res_copies)

    lane = lax.broadcasted_iota(jnp.int32, (GRP, 128), 1)
    trow = lax.broadcasted_iota(jnp.int32, (GRP, 128), 0)
    pos = lane % SEQ
    quad = 128 // SEQ
    in_group = (lane // SEQ) == (trow % quad)
    tgrp = trow // quad
    NG = GRP // quad
    scale = HD ** -0.5

    def attend(c, b, slot):
        for g in range(KV_TOK // GRP):
            r0 = pl.multiple_of(b * KV_TOK + g * GRP, GRP)
            rr = pl.ds(r0, GRP)
            tr = pl.ds(pl.multiple_of(c * M + b * KV_TOK + g * GRP, GRP), GRP)
            co, si = cos_t[tr, :], sin_t[tr, :]
            ok = jnp.logical_and(in_group, pos < lens[tr, :])

            def rot(z):
                zf = z.astype(F32)
                return (zf * co + pltpu.roll(zf, HD // 2, 1) * si).astype(BF16)

            kr = rot(qk[rr, pl.ds(QW, HD)]).astype(F32)
            qs = jnp.concatenate([rot(qk[rr, pl.ds(h * HD, HD)]) for h in range(NH)], axis=0)
            vn = vnew[rr, :].astype(F32)
            kb = kbuf[slot, pl.ds(g * GRP, GRP)].reshape(GRP * SEQ, HD)
            vb = vbuf[slot, pl.ds(g * GRP, GRP)].reshape(GRP * SEQ, HD)
            s = lax.dot_general(qs, kb, (((1,), (1,)), ((), ())), preferred_element_type=F32)
            s = s.reshape(NH, GRP, GRP * SEQ)
            lg = s[:, :, 0:128]
            for n in range(1, NG):
                lg = jnp.where((tgrp == n)[None], s[:, :, n * 128:(n + 1) * 128], lg)
            lg = jnp.where(ok[None], lg * scale, -jnp.inf)
            self_l = jnp.sum(qs.reshape(NH, GRP, HD).astype(F32) * kr[None], axis=-1, keepdims=True) * scale
            peak = jnp.maximum(jnp.max(lg, axis=-1, keepdims=True), self_l)
            w = jnp.exp(lg - peak)
            ws = jnp.exp(self_l - peak)
            den = jnp.sum(w, axis=-1, keepdims=True) + ws
            p = w / den
            ps = (ws / den).astype(BF16).astype(F32)
            pe = jnp.concatenate([jnp.where((tgrp == n)[None], p, 0.0) for n in range(NG)], axis=-1)
            pe = pe.astype(BF16).reshape(NH * GRP, GRP * SEQ)
            o = jnp.dot(pe, vb, preferred_element_type=F32).reshape(NH, GRP, HD)
            o = (o + ps * vn[None]).astype(BF16)
            for h in range(NH):
                hid[rr, pl.ds(h * HD, HD)] = o[h]

    def glu(gate, up):
        gf = gate.astype(BF16).astype(F32)
        uf = up.astype(BF16).astype(F32)
        return (gf * jax.nn.sigmoid(gf) * uf).astype(BF16)

    def dot(a, b):
        return jnp.dot(a, b, preferred_element_type=F32)

    def body(it, carry):
        l = it // CHUNKS
        c = it % CHUNKS
        pc = (it + CHUNKS - 1) % CHUNKS
        plr = (it + CHUNKS - 1) // CHUNKS - 1
        nl = (it + 1) // CHUNKS
        nc = (it + 1) % CHUNKS

        @pl.when(it == 1)
        def _():
            first_norm(1)

        @pl.when(it >= CHUNKS)
        def _():
            gathered(c)

        start(dn_copies(l, 0, 0))
        wait(qk_copies(l))
        start(gu_copies(l, 0, 1))
        for n in range((QW + HD) // SUB):
            qk[:, pl.ds(n * SUB, SUB)] = dot(act[c], w1[0, :, pl.ds(n * SUB, SUB)]).astype(BF16)
        wait(sp_copies(l))
        r = dot(act[c], wsp[...])
        vnew[...] = r[:, :HD].astype(BF16)
        hid[:, pl.ds(QW + GU_N * GU_TILE, REM)] = glu(r[:, HD:HD + REM], r[:, HD + REM:])
        start(dn_copies(l, 1, 1))

        def att_step(b, carry):
            slot = b % 2

            @pl.when(b + 1 < KV_N)
            def _():
                start(kv_copies(l, c, b + 1, 1 - slot))

            wait(kv_copies(l, c, b, slot))
            attend(c, b, slot)
            return carry

        lax.fori_loop(0, KV_N, att_step, 0)

        def gu_step(j, carry):
            slot = (j + 1) % 2

            @pl.when(j + 1 < GU_N)
            def _():
                start(gu_copies(l, j + 1, 1 - slot))

            @pl.when(jnp.logical_and(j + 1 == GU_N, it + 1 < iters))
            def _():
                start(qk_copies(nl))
                start(sp_copies(nl))
                start(kv_copies(nl, nc, 0, 0))

            @pl.when(jnp.logical_and(j == HOOK_SUM, it > 0))
            def _():
                sum_and_send(plr, pc)

            wait(gu_copies(l, j, slot))
            for n in range(GU_TILE // SUB):
                g = dot(act[c], w1[slot, :, pl.ds(n * SUB, SUB)])
                u = dot(act[c], w1[slot, :, pl.ds(GU_TILE + n * SUB, SUB)])
                hid[:, pl.ds(pl.multiple_of(QW + j * GU_TILE + n * SUB, 128), SUB)] = glu(g, u)
            return carry

        lax.fori_loop(0, GU_N, gu_step, 0)

        @pl.when(it > 0)
        def _():
            for k in range(3):
                share_all(pc, k).wait_send()

        def dn_step(j, carry):
            slot = j % 2

            @pl.when(jnp.logical_and(j == HOOK_FWD, it > 0))
            def _():
                forward(pc)

            wait(dn_copies(l, j, slot))

            @pl.when(j > 0)
            def _():
                for k in (1, 2, 0):
                    share_copy(c, k, j - 1).start()

            for n in range(DN_TILE // SUB):
                share[:, pl.ds(pl.multiple_of(j * DN_TILE + n * SUB, SUB), SUB)] = dot(
                    hid[...], w2[slot, :, pl.ds(n * SUB, SUB)]).astype(BF16)

            @pl.when(j + 2 < DN_N)
            def _():
                start(dn_copies(l, j + 2, slot))
            return carry

        lax.fori_loop(0, DN_N, dn_step, 0)
        for k in (1, 2, 0):
            share_copy(c, k, DN_N - 1).start()
        return carry

    lax.fori_loop(0, iters, body, 0)

    fc = (iters - 1) % CHUNKS
    outs = []
    for c in [(iters - CHUNKS + i) % CHUNKS for i in range(CHUNKS)]:
        if c == fc:
            sum_and_send(jnp.int32(L - 1), fc)
            for k in range(3):
                share_all(fc, k).wait_send()
            forward(fc)
        gathered(c)
        cp = pltpu.make_async_copy(act.at[c], out.at[pl.ds(c * M, M)], io_sem.at[c])
        cp.start()
        outs.append(cp)
    wait(outs)


def solution(mesh):
    tp_size = mesh.shape['tp']
    arg_specs = (P('dp', None), P('dp'), P(), P(None, None, 'tp'), P(None, None, 'tp'), P(None, None, 'tp'), P(None, 'tp', None), P(None, None, 'tp'), P(None, None, 'tp'), P(None, 'tp', None), P(None, 'dp', None, 'tp', None), P(None, 'dp', None, 'tp', None))

    def per_device(x_in, lengths, norm_gain, w_q, w_k, w_v, w_o, w_gate, w_up, w_down, k_cache, v_cache):
        L, tok, seq, kvh, hd = k_cache.shape
        D = x_in.shape[1]
        qw = w_q.shape[2]
        ff = w_gate.shape[2]
        inv_freq = 1.0 / (ROPE_BASE ** (jnp.arange(0, hd, 2).astype(F32) / hd))
        ang = lengths.astype(F32)[:, None] * inv_freq[None, :]
        cos, sin = jnp.cos(ang), jnp.sin(ang)
        cos_t = jnp.concatenate([cos, cos], axis=-1)
        sin_t = jnp.concatenate([-sin, sin], axis=-1)
        lens = jnp.broadcast_to(lengths[:, None], (tok, 128))
        kc = k_cache.reshape(L, tok, seq, hd)
        vc = v_cache.reshape(L, tok, seq, hd)
        M = tok // CHUNKS
        Q = M // tp_size
        vmem = pl.BlockSpec(memory_space=pltpu.VMEM)
        hbm = pl.BlockSpec(memory_space=pl.ANY)
        dma = pltpu.SemaphoreType.DMA
        rem = ff - (ff // GU_TILE) * GU_TILE
        return pl.pallas_call(
            functools.partial(layers_kernel, tp_size, (L, tok, D, qw, hd, ff, seq)),
            out_shape=jax.ShapeDtypeStruct((tok, D), BF16),
            in_specs=[hbm, vmem, vmem, vmem, vmem] + [hbm] * 9,
            out_specs=hbm,
            scratch_shapes=[
                pltpu.VMEM((CHUNKS, M, D), BF16),
                pltpu.VMEM((2, D, 2 * GU_TILE), BF16),
                pltpu.VMEM((D, hd + 2 * rem), BF16),
                pltpu.VMEM((2, qw + ff, DN_TILE), BF16),
                pltpu.VMEM((M, qw + ff), BF16),
                pltpu.VMEM((M, qw + hd), BF16),
                pltpu.VMEM((M, hd), BF16),
                pltpu.VMEM((2, KV_TOK, seq, hd), BF16),
                pltpu.VMEM((2, KV_TOK, seq, hd), BF16),
                pltpu.VMEM((M, D), BF16),
                pltpu.VMEM((CHUNKS, 3, Q, D), BF16),
                pltpu.VMEM((CHUNKS, Q, D), BF16),
                dma((2, 2)), dma((3,)), dma((2, 2)), dma((2, 2)), dma((2 * CHUNKS,)),
                dma((3,)), dma((CHUNKS, 3)), dma((CHUNKS, 3)), dma((CHUNKS, 3)),
            ],
            compiler_params=pltpu.CompilerParams(
                collective_id=0, has_side_effects=True, vmem_limit_bytes=67043328),
            name="layers",
        )(x_in, lens, cos_t, sin_t, norm_gain.astype(F32).reshape(L, 1, D), w_q, w_k, w_v, w_o, w_gate, w_up, w_down, kc, vc)

    return jax.shard_map(per_device, mesh=mesh, in_specs=arg_specs, out_specs=P('dp', None), check_vma=False)
```

time: 824 us -> 387 us (0.47)
  matrix products: 376 us -> 0 us
  Pallas kernels: 0 us -> 374 us
  waiting for transfers between devices: 185 us -> 0 us
  other arithmetic: 101 us -> 3.93 us
  blocking collectives: 85.4 us -> 0 us
  local copies, waits for them, and re-layouts: 51.4 us -> 9.63 us
  between operations: 14.3 us -> 0.02 us
    dot_general x18 -> x0, matrix products: 376 us -> none  [the longest x2 94.7 us: layer_update(): jnp.dot(normed, wg_layer, preferred_element_type=jnp.float32)]
    pallas_call x0 -> x1, Pallas kernels: none -> 374 us  [per_device(): pl.pallas_call(functools.partial(layers_kernel, tp_size, (L, tok, D, qw,...]
    all_gather x2 -> x0, waiting for transfers between devices: 102 us -> none  [per_device(): x_res = lax.all_gather(new_cols, 'tp', axis=1, tiled=True)]
    all_to_all x1 -> x0, blocking collectives: 85.4 us -> none  [per_device(): received = lax.all_to_all(partial_sum, 'tp', 1, 0, tiled=True)]
    all_to_all x1 -> x0, waiting for transfers between devices: 82.5 us -> none  [per_device(): received = lax.all_to_all(partial_sum, 'tp', 1, 0, tiled=True)]
    reduce_sum x6 -> x0, other arithmetic: 50.7 us -> none  [the longest x2 32 us: decode_attention(): prob_denom = jnp.sum(cache_w, axis=-1) + self_w]
    dot_general x2 -> x0, other arithmetic: 19.8 us -> none  [layer_update(): jnp.dot(mlp_hidden, wd_layer, preferred_element_type=jnp.float32)]
    unnamed x69 -> x1, local copies, waits for them, and re-layouts: 24.8 us -> 6.6 us
  transfers between devices with their start and end apart: 3 -> 0, of which waited for: 3 -> 0; matrix products, arithmetic and copies ran while one was open for 0% -> 0% of each run, Pallas kernels for 0% -> 0%
where the time goes in v1:
time: 387 us
  Pallas kernels  374 us (97%)
  local copies, waits for them, and re-layouts  9.63 us (2%)
  other arithmetic  3.93 us (1%)
    pallas_call x1, Pallas kernels, per_device(): pl.pallas_call(functools.partial(layers_kernel, tp_size, (L, tok, D, qw,...  374 us

profile of v1, /device:TPU:0, one launch (start us, length us, event | category | flops | bytes accessed | tf_op | source)
XLA Modules:
  0.0 387.2 jit_solution(393512829541207157)
XLA Ops:
  0.0 0.7 convert_element_type.11
  0.7 1.3 reshape.26.refs_4_
  2.0 1.7 broadcast_in_dim.2.refs_1_
  3.7 1.9 fusion
  5.6 1.3 pad_maximum_fusion
  7.0 373.7 %layers.1 = bf16[1024,3584]{1,0:T(8,128)(2,1)} custom-call(bf16[1024,3584]{1,0:T(8,128)(2,1)} %refs_0_.1, s32[1024,128]{1,0:T(8,128)} %broadcast_in_dim.2.refs_1_, f32[1024,128]{1,0:T(8,128)} %get-tuple-element.8.refs_2_, f32[1024,128]{1,0:T(8,128)} %get-tuple-element.9.refs_3_, f32[2,1,3584]{2,1,0:T(1,128)} %reshape.26.refs_4_, ...), custom_call_target="tpu_custom_call" | custom-call | tf_op jit(solution)/shard_map/layers/pallas_call | solution.py:372
  380.6 6.6 %copy.14 = bf16[1024,3584]{1,0:T(8,128)(2,1)} copy(bf16[1024,3584]{1,0:T(8,128)(2,1)} %layers.1) | data formatting | bytes 14680064
  (1 shorter events, 0.0 us)

commit v2 on v1

--- a/solution.py
+++ b/solution.py
@@ -20,14 +20,15 @@
 KV_TOK = 64
 GRP = 16
 ROWS = 16
+UNROLL = 2
 HOOK_SUM = 5
-HOOK_FWD = 2
+HOOK_FWD = 3
 
 
 def layers_kernel(tp, dims, *refs):
-    (x_in, lens, cos_t, sin_t, gain, wq, wk, wv, wo, wg, wu, wd, kc, vc, out,
-     act, w1, wsp, w2, hid, qk, vnew, kbuf, vbuf, share, recv, xres,
-     w1_sem, wsp_sem, w2_sem, kv_sem, io_sem, rs_send, rs_recv, ag_send, ag_recv) = refs
+    (x_in, lens, cs_t, gain, wq, wk, wv, wo, wg, wu, wd, kc, vc, out,
+     act, w1, wsp, w2, hid, qk, vnew, kbuf, vbuf, share, recv, xres, logit, selfp, prob,
+     w1_sem, wsp_sem, w2_sem, kv_sem, io_sem, rs_send, rs_recv, ag_send, ag_recv, fin_send, fin_recv) = refs
     L, tok, D, QW, HD, FF, SEQ = dims
     M = tok // CHUNKS
     Q = M // tp
@@ -36,6 +37,8 @@
     GU_N = FF // GU_TILE
     REM = FF - GU_N * GU_TILE
     DN_N = D // DN_TILE
+    PIECES = D // SUB
+    PER = DN_TILE // SUB
     KV_N = M // KV_TOK
 
     me = lax.axis_index("tp")
@@ -83,17 +86,24 @@
         for cp in copies:
             cp.wait()
 
+    def piece(p):
+        return pl.ds(pl.multiple_of(p * SUB, SUB), SUB)
+
     def share_copy(c, k, j):
-        cols = pl.ds(pl.multiple_of(j * DN_TILE, DN_TILE), DN_TILE)
+        cols = piece(j)
         return pltpu.make_async_remote_copy(
             src_ref=share.at[rows_of(peers[k]), cols], dst_ref=recv.at[c, k, :, cols],
-            send_sem=rs_send.at[k], recv_sem=rs_recv.at[c, k],
+            send_sem=rs_send.at[k], recv_sem=rs_recv.at[c, k, j],
             device_id={"tp": peers[k]}, device_id_type=MESH)
+
+    def send_piece(c, j):
+        for k in (1, 2, 0):
+            share_copy(c, k, j).start()
 
     def share_all(c, k):
         return pltpu.make_async_remote_copy(
             src_ref=share.at[rows_of(peers[k])], dst_ref=recv.at[c, k],
-            send_sem=rs_send.at[k], recv_sem=rs_recv.at[c, k],
+            send_sem=rs_send.at[k], recv_sem=rs_recv.at[c, k, 0],
             device_id={"tp": peers[k]}, device_id_type=MESH)
 
     def gather_copy(c, k):
@@ -104,35 +114,46 @@
             send_sem=ag_send.at[c, k], recv_sem=ag_recv.at[c, k],
             device_id={"tp": to}, device_id_type=MESH)
 
+    def gain_row(l):
+        rows = gain[...].astype(F32)
+        row = rows[0:1]
+        for i in range(1, L):
+            row = jnp.where(l >= i, rows[i:i + 1], row)
+        return row
+
     def normed(xf, grow):
         inv = lax.rsqrt(jnp.mean(xf * xf, axis=-1, keepdims=True) + NORM_EPS)
-        return (xf * inv * grow).astype(BF16)
+        return xf * inv * grow
+
+    def groups_of(r, base):
+        return [pl.ds(pl.multiple_of(base + (r * UNROLL + i) * ROWS, ROWS), ROWS) for i in range(UNROLL)]
 
     def sum_and_send(l, c):
-        for k in range(3):
-            share_all(c, k).wait_recv()
+        def arrived(j, carry):
+            for k in range(3):
+                share_copy(c, k, j).wait_recv()
+            return carry
+
+        lax.fori_loop(0, PIECES, arrived, 0)
         last = l == L - 1
-        grow = gain[jnp.minimum(l + 1, L - 1)]
+        grow = gain_row(l + 1)
 
         def step(r, carry):
-            rr = pl.ds(pl.multiple_of(r * ROWS, ROWS), ROWS)
-            own = pl.ds(pl.multiple_of(me * Q + r * ROWS, ROWS), ROWS)
-            s = share[own, :].astype(F32)
-            for k in range(3):
-                s = s + recv[c, k, rr, :].astype(F32)
-            xn = (xres[c, rr, :].astype(F32) + s).astype(BF16)
-            xres[c, rr, :] = xn
-
-            @pl.when(last)
-            def _():
-                act[c, own, :] = xn
-
-            @pl.when(jnp.logical_not(last))
-            def _():
-                act[c, own, :] = normed(xn.astype(F32), grow)
+            rows, owns = groups_of(r, 0), groups_of(r, me * Q)
+            new = []
+            for rr, own in zip(rows, owns):
+                s = share[own, :].astype(F32)
+                for k in range(3):
+                    s = s + recv[c, k, rr, :].astype(F32)
+                xn = (xres[c, rr, :].astype(F32) + s).astype(BF16)
+                xf = xn.astype(F32)
+                new.append((xn, jnp.where(last, xf, normed(xf, grow)).astype(BF16)))
+            for rr, own, (xn, a) in zip(rows, owns, new):
+                xres[c, rr, :] = xn
+                act[c, own, :] = a
             return carry
 
-        lax.fori_loop(0, Q // ROWS, step, 0)
+        lax.fori_loop(0, Q // (ROWS * UNROLL), step, 0)
         gather_copy(c, 1).start()
         gather_copy(c, 0).start()
 
@@ -161,17 +182,19 @@
         pl.semaphore_signal(barrier, inc=1, device_id={"tp": p}, device_id_type=MESH)
     pl.semaphore_wait(barrier, 3)
 
-    grow0 = gain[0]
+    grow0 = gain_row(0)
 
     def first_norm(c):
         x_copies[c].wait()
 
         def step(r, carry):
-            rr = pl.ds(pl.multiple_of(r * ROWS, ROWS), ROWS)
-            act[c, rr, :] = normed(act[c, rr, :].astype(F32), grow0)
+            rows = groups_of(r, 0)
+            new = [normed(act[c, rr, :].astype(F32), grow0).astype(BF16) for rr in rows]
+            for rr, a in zip(rows, new):
+                act[c, rr, :] = a
             return carry
 
-        lax.fori_loop(0, M // ROWS, step, 0)
+        lax.fori_loop(0, M // (ROWS * UNROLL), step, 0)
 
     first_norm(0)
     wait(res_copies)
@@ -185,42 +208,55 @@
     NG = GRP // quad
     scale = HD ** -0.5
 
-    def attend(c, b, slot):
-        for g in range(KV_TOK // GRP):
-            r0 = pl.multiple_of(b * KV_TOK + g * GRP, GRP)
-            rr = pl.ds(r0, GRP)
-            tr = pl.ds(pl.multiple_of(c * M + b * KV_TOK + g * GRP, GRP), GRP)
-            co, si = cos_t[tr, :], sin_t[tr, :]
-            ok = jnp.logical_and(in_group, pos < lens[tr, :])
-
-            def rot(z):
-                zf = z.astype(F32)
-                return (zf * co + pltpu.roll(zf, HD // 2, 1) * si).astype(BF16)
-
-            kr = rot(qk[rr, pl.ds(QW, HD)]).astype(F32)
-            qs = jnp.concatenate([rot(qk[rr, pl.ds(h * HD, HD)]) for h in range(NH)], axis=0)
-            vn = vnew[rr, :].astype(F32)
-            kb = kbuf[slot, pl.ds(g * GRP, GRP)].reshape(GRP * SEQ, HD)
-            vb = vbuf[slot, pl.ds(g * GRP, GRP)].reshape(GRP * SEQ, HD)
-            s = lax.dot_general(qs, kb, (((1,), (1,)), ((), ())), preferred_element_type=F32)
-            s = s.reshape(NH, GRP, GRP * SEQ)
-            lg = s[:, :, 0:128]
-            for n in range(1, NG):
-                lg = jnp.where((tgrp == n)[None], s[:, :, n * 128:(n + 1) * 128], lg)
-            lg = jnp.where(ok[None], lg * scale, -jnp.inf)
-            self_l = jnp.sum(qs.reshape(NH, GRP, HD).astype(F32) * kr[None], axis=-1, keepdims=True) * scale
-            peak = jnp.maximum(jnp.max(lg, axis=-1, keepdims=True), self_l)
-            w = jnp.exp(lg - peak)
-            ws = jnp.exp(self_l - peak)
-            den = jnp.sum(w, axis=-1, keepdims=True) + ws
-            p = w / den
-            ps = (ws / den).astype(BF16).astype(F32)
-            pe = jnp.concatenate([jnp.where((tgrp == n)[None], p, 0.0) for n in range(NG)], axis=-1)
-            pe = pe.astype(BF16).reshape(NH * GRP, GRP * SEQ)
-            o = jnp.dot(pe, vb, preferred_element_type=F32).reshape(NH, GRP, HD)
-            o = (o + ps * vn[None]).astype(BF16)
-            for h in range(NH):
-                hid[rr, pl.ds(h * HD, HD)] = o[h]
+    first_half = lane < HD // 2
+    groups = range(KV_TOK // GRP)
+
+    def toks(base, b, g):
+        return pl.ds(pl.multiple_of(base + b * KV_TOK + g * GRP, GRP), GRP)
+
+    def attend_scores(c, b, slot, g):
+        rr, tr = toks(0, b, g), toks(c * M, b, g)
+        cs = cs_t[tr, :]
+        sc = pltpu.roll(cs, HD // 2, 1)
+        co = jnp.where(first_half, cs, sc)
+        si = jnp.where(first_half, -sc, cs)
+
+        def rot(z):
+            zf = z.astype(F32)
+            return (zf * co + pltpu.roll(zf, HD // 2, 1) * si).astype(BF16)
+
+        kr = rot(qk[rr, pl.ds(QW, HD)]).astype(F32)
+        qs = jnp.concatenate([rot(qk[rr, pl.ds(h * HD, HD)]) for h in range(NH)], axis=0)
+        kb = kbuf[slot, pl.ds(g * GRP, GRP)].reshape(GRP * SEQ, HD)
+        s = lax.dot_general(qs, kb, (((1,), (1,)), ((), ())), preferred_element_type=F32)
+        s = s.reshape(NH, GRP, GRP * SEQ)
+        lg = s[:, :, 0:128]
+        for n in range(1, NG):
+            lg = jnp.where((tgrp == n)[None], s[:, :, n * 128:(n + 1) * 128], lg)
+        ok = jnp.logical_and(in_group, pos < lens[tr, :])
+        logit[g] = jnp.where(ok[None], lg * scale, -jnp.inf)
+        selfl = jnp.sum(qs.reshape(NH, GRP, HD).astype(F32) * kr[None], axis=-1, keepdims=True) * scale
+        selfp[g] = jnp.broadcast_to(selfl, (NH, GRP, HD))
+
+    def attend_softmax(g):
+        lg = logit[g]
+        self_l = selfp[g]
+        peak = jnp.maximum(jnp.max(lg, axis=-1, keepdims=True), self_l)
+        w = jnp.exp(lg - peak)
+        ws = jnp.exp(self_l - peak)
+        den = jnp.sum(w, axis=-1, keepdims=True) + ws
+        p = w / den
+        selfp[g] = (ws / den).astype(BF16).astype(F32)
+        pe = jnp.concatenate([jnp.where((tgrp == n)[None], p, 0.0) for n in range(NG)], axis=-1)
+        prob[g] = pe.astype(BF16).reshape(NH * GRP, GRP * SEQ)
+
+    def attend_values(b, slot, g):
+        rr = toks(0, b, g)
+        vb = vbuf[slot, pl.ds(g * GRP, GRP)].reshape(GRP * SEQ, HD)
+        o = jnp.dot(prob[g], vb, preferred_element_type=F32).reshape(NH, GRP, HD)
+        o = (o + selfp[g] * vnew[rr, :].astype(F32)[None]).astype(BF16)
+        for h in range(NH):
+            hid[rr, pl.ds(h * HD, HD)] = o[h]
 
     def glu(gate, up):
         gf = gate.astype(BF16).astype(F32)
@@ -257,21 +293,14 @@
         hid[:, pl.ds(QW + GU_N * GU_TILE, REM)] = glu(r[:, HD:HD + REM], r[:, HD + REM:])
         start(dn_copies(l, 1, 1))
 
-        def att_step(b, carry):
-            slot = b % 2
-
-            @pl.when(b + 1 < KV_N)
-            def _():
-                start(kv_copies(l, c, b + 1, 1 - slot))
-
-            wait(kv_copies(l, c, b, slot))
-            attend(c, b, slot)
-            return carry
-
-        lax.fori_loop(0, KV_N, att_step, 0)
-
-        def gu_step(j, carry):
+        def gu_step(j, carry, attend):
             slot = (j + 1) % 2
+            kvs = j % 2
+
+            if attend:
+                @pl.when(j + 1 < KV_N)
+                def _():
+                    start(kv_copies(l, c, j + 1, 1 - kvs))
 
             @pl.when(j + 1 < GU_N)
             def _():
@@ -288,13 +317,22 @@
                 sum_and_send(plr, pc)
 
             wait(gu_copies(l, j, slot))
+            if attend:
+                wait(kv_copies(l, c, j, kvs))
+            stages = [lambda g: attend_scores(c, j, kvs, g), attend_softmax, lambda g: attend_values(j, kvs, g)]
             for n in range(GU_TILE // SUB):
-                g = dot(act[c], w1[slot, :, pl.ds(n * SUB, SUB)])
-                u = dot(act[c], w1[slot, :, pl.ds(GU_TILE + n * SUB, SUB)])
-                hid[:, pl.ds(pl.multiple_of(QW + j * GU_TILE + n * SUB, 128), SUB)] = glu(g, u)
+                gu = []
+                for half_cols in (0, GU_TILE):
+                    gu.append(dot(act[c], w1[slot, :, pl.ds(half_cols + n * SUB, SUB)]))
+                    if attend and stages:
+                        stage = stages.pop(0)
+                        for g in groups:
+                            stage(g)
+                hid[:, pl.ds(pl.multiple_of(QW + j * GU_TILE + n * SUB, 128), SUB)] = glu(*gu)
             return carry
 
-        lax.fori_loop(0, GU_N, gu_step, 0)
+        lax.fori_loop(0, KV_N, functools.partial(gu_step, attend=True), 0)
+        lax.fori_loop(KV_N, GU_N, functools.partial(gu_step, attend=False), 0)
 
         @pl.when(it > 0)
         def _():
@@ -310,40 +348,87 @@
 
             wait(dn_copies(l, j, slot))
 
-            @pl.when(j > 0)
-            def _():
-                for k in (1, 2, 0):
-                    share_copy(c, k, j - 1).start()
-
-            for n in range(DN_TILE // SUB):
+            for n in range(PER):
                 share[:, pl.ds(pl.multiple_of(j * DN_TILE + n * SUB, SUB), SUB)] = dot(
                     hid[...], w2[slot, :, pl.ds(n * SUB, SUB)]).astype(BF16)
 
             @pl.when(j + 2 < DN_N)
             def _():
                 start(dn_copies(l, j + 2, slot))
+
+            @pl.when(j > 0)
+            def _():
+                send_piece(c, j * PER - 1)
+
+            for n in range(PER - 1):
+                send_piece(c, j * PER + n)
             return carry
 
         lax.fori_loop(0, DN_N, dn_step, 0)
-        for k in (1, 2, 0):
-            share_copy(c, k, DN_N - 1).start()
+        send_piece(c, PIECES - 1)
         return carry
 
     lax.fori_loop(0, iters, body, 0)
 
     fc = (iters - 1) % CHUNKS
-    outs = []
-    for c in [(iters - CHUNKS + i) % CHUNKS for i in range(CHUNKS)]:
-        if c == fc:
-            sum_and_send(jnp.int32(L - 1), fc)
+
+    def final_copy(k, j):
+        block = rows_of(cross) if k == 2 else my_rows
+        return pltpu.make_async_remote_copy(
+            src_ref=act.at[fc, block, piece(j)], dst_ref=act.at[fc, block, piece(j)],
+            send_sem=fin_send.at[k], recv_sem=fin_recv.at[k, j],
+            device_id={"tp": cross if k == 1 else sib}, device_id_type=MESH)
+
+    def out_copy(j):
+        return pltpu.make_async_copy(
+            act.at[fc, :, piece(j)], out.at[pl.ds(fc * M, M), piece(j)], io_sem.at[fc])
+
+    out_copies = []
+    for c in range(CHUNKS):
+        if c != fc:
+            gathered(c)
+            cp = pltpu.make_async_copy(act.at[c], out.at[pl.ds(c * M, M)], io_sem.at[c])
+            cp.start()
+            out_copies.append(cp)
+
+    def final_sum(j, carry):
+        for k in range(3):
+            share_copy(fc, k, j).wait_recv()
+        for r in range(0, Q, ROWS):
+            own = pl.ds(pl.multiple_of(me * Q + r, ROWS), ROWS)
+            t = share[own, piece(j)].astype(F32)
             for k in range(3):
-                share_all(fc, k).wait_send()
-            forward(fc)
-        gathered(c)
-        cp = pltpu.make_async_copy(act.at[c], out.at[pl.ds(c * M, M)], io_sem.at[c])
-        cp.start()
-        outs.append(cp)
-    wait(outs)
+                t = t + recv[fc, k, pl.ds(r, ROWS), piece(j)].astype(F32)
+            act[fc, own, piece(j)] = (xres[fc, pl.ds(r, ROWS), piece(j)].astype(F32) + t).astype(BF16)
+        final_copy(1, j).start()
+        final_copy(0, j).start()
+        return carry
+
+    lax.fori_loop(0, PIECES, final_sum, 0)
+
+    def final_forward(j, carry):
+        @pl.when(j < PIECES)
+        def _():
+            final_copy(1, j).wait_recv()
+            final_copy(2, j).start()
+
+        @pl.when(j > 0)
+        def _():
+            final_copy(0, j - 1).wait_recv()
+            final_copy(2, j - 1).wait_recv()
+            out_copy(j - 1).start()
+        return carry
+
+    lax.fori_loop(0, PIECES + 1, final_forward, 0)
+    for k in range(3):
+        share_all(fc, k).wait_send()
+        block = rows_of(cross) if k == 2 else my_rows
+        pltpu.make_async_remote_copy(
+            src_ref=act.at[fc, block], dst_ref=act.at[fc, block], send_sem=fin_send.at[k],
+            recv_sem=fin_recv.at[k, 0], device_id={"tp": cross if k == 1 else sib},
+            device_id_type=MESH).wait_send()
+    pltpu.make_async_copy(act.at[fc], out.at[pl.ds(fc * M, M)], io_sem.at[fc]).wait()
+    wait(out_copies)
 
 
 def solution(mesh):
@@ -357,9 +442,7 @@
         ff = w_gate.shape[2]
         inv_freq = 1.0 / (ROPE_BASE ** (jnp.arange(0, hd, 2).astype(F32) / hd))
         ang = lengths.astype(F32)[:, None] * inv_freq[None, :]
-        cos, sin = jnp.cos(ang), jnp.sin(ang)
-        cos_t = jnp.concatenate([cos, cos], axis=-1)
-        sin_t = jnp.concatenate([-sin, sin], axis=-1)
+        cs_t = jnp.concatenate([jnp.cos(ang), jnp.sin(ang)], axis=-1)
         lens = jnp.broadcast_to(lengths[:, None], (tok, 128))
         kc = k_cache.reshape(L, tok, seq, hd)
         vc = v_cache.reshape(L, tok, seq, hd)
@@ -372,7 +455,7 @@
         return pl.pallas_call(
             functools.partial(layers_kernel, tp_size, (L, tok, D, qw, hd, ff, seq)),
             out_shape=jax.ShapeDtypeStruct((tok, D), BF16),
-            in_specs=[hbm, vmem, vmem, vmem, vmem] + [hbm] * 9,
+            in_specs=[hbm, vmem, vmem, vmem] + [hbm] * 9,
             out_specs=hbm,
             scratch_shapes=[
                 pltpu.VMEM((CHUNKS, M, D), BF16),
@@ -387,12 +470,16 @@
                 pltpu.VMEM((M, D), BF16),
                 pltpu.VMEM((CHUNKS, 3, Q, D), BF16),
                 pltpu.VMEM((CHUNKS, Q, D), BF16),
+                pltpu.VMEM((KV_TOK // GRP, qw // hd, GRP, hd), F32),
+                pltpu.VMEM((KV_TOK // GRP, qw // hd, GRP, hd), F32),
+                pltpu.VMEM((KV_TOK // GRP, qw // hd * GRP, GRP * seq), BF16),
                 dma((2, 2)), dma((3,)), dma((2, 2)), dma((2, 2)), dma((2 * CHUNKS,)),
-                dma((3,)), dma((CHUNKS, 3)), dma((CHUNKS, 3)), dma((CHUNKS, 3)),
+                dma((3,)), dma((CHUNKS, 3, D // SUB)), dma((CHUNKS, 3)), dma((CHUNKS, 3)),
+                dma((3,)), dma((3, D // SUB)),
             ],
             compiler_params=pltpu.CompilerParams(
                 collective_id=0, has_side_effects=True, vmem_limit_bytes=67043328),
             name="layers",
-        )(x_in, lens, cos_t, sin_t, norm_gain.astype(F32).reshape(L, 1, D), w_q, w_k, w_v, w_o, w_gate, w_up, w_down, kc, vc)
+        )(x_in, lens, cs_t, norm_gain, w_q, w_k, w_v, w_o, w_gate, w_up, w_down, kc, vc)
 
     return jax.shard_map(per_device, mesh=mesh, in_specs=arg_specs, out_specs=P('dp', None), check_vma=False)

time: 387 us -> 342 us (0.88)
  Pallas kernels: 374 us -> 330 us
    pallas_call x1, Pallas kernels: 374 us -> 330 us  [per_device(): pl.pallas_call(functools.partial(layers_kernel, tp_size, (L, tok, D, qw,...]
where the time goes in v2:
time: 342 us; the launch traced here: 341 us
  Pallas kernels  330 us (96%)
  local copies, waits for them, and re-layouts  8.28 us (2%)
  other arithmetic  3.57 us (1%)
    pallas_call x1, Pallas kernels, per_device(): pl.pallas_call(functools.partial(layers_kernel, tp_size, (L, tok, D, qw,...  330 us

profile of v2, /device:TPU:0, one launch (start us, length us, event | category | flops | bytes accessed | tf_op | source)
XLA Modules:
  0.0 341.4 jit_solution(15533141179968748436)
XLA Ops:
  0.0 0.7 convert_element_type.10
  0.7 1.7 broadcast_in_dim.2.refs_1_
  2.4 1.9 multiply_cosine_fusion
  4.3 1.0 pad_maximum_fusion.refs_2_
  5.3 329.5 %layers.1 = bf16[1024,3584]{1,0:T(8,128)(2,1)} custom-call(bf16[1024,3584]{1,0:T(8,128)(2,1)} %refs_0_.1, s32[1024,128]{1,0:T(8,128)} %broadcast_in_dim.2.refs_1_, f32[1024,128]{1,0:T(8,128)} %pad_maximum_fusion.refs_2_, bf16[2,3584]{1,0:T(2,128)(2,1)} %refs_3_.1, bf16[2,3584,896]{2,1,0:T(8,128)(2,1)} %refs_4_.1, bf16[2,3584,128]{2,1,0:T(8,128)(2,1)} %refs_5_.1, ...), custom_call_target="tpu_custom_call" | custom-call | tf_op jit(solution)/shard_map/layers/pallas_call | solution.py:455
  334.8 6.6 %copy.14 = bf16[1024,3584]{1,0:T(8,128)(2,1)} copy(bf16[1024,3584]{1,0:T(8,128)(2,1)} %layers.1) | data formatting | bytes 14680064
  (1 shorter events, 0.0 us)

commit v3 on v2

--- a/solution.py
+++ b/solution.py
@@ -26,9 +26,10 @@
 
 
 def layers_kernel(tp, dims, *refs):
-    (x_in, lens, cs_t, gain, wq, wk, wv, wo, wg, wu, wd, kc, vc, out,
-     act, w1, wsp, w2, hid, qk, vnew, kbuf, vbuf, share, recv, xres, logit, selfp, prob,
-     w1_sem, wsp_sem, w2_sem, kv_sem, io_sem, rs_send, rs_recv, ag_send, ag_recv, fin_send, fin_recv) = refs
+    (x_in, lens, cs_t, gain, wq, wk, wv, wo, wg, wu, wd, kc, vc, out, wx,
+     act, w1, w2, hid, qk, vnew, kbuf, vbuf, share, recv, xres, logit, selfp, prob, hsib,
+     w1_sem, wsp_sem, w2_sem, kv_sem, io_sem, rs_send, rs_recv, ag_send, ag_recv, fin_send, fin_recv,
+     wx_sem, hx_sem, xx_sem) = refs
     L, tok, D, QW, HD, FF, SEQ = dims
     M = tok // CHUNKS
     Q = M // tp
@@ -39,6 +40,12 @@
     DN_N = D // DN_TILE
     PIECES = D // SUB
     PER = DN_TILE // SUB
+    HC = D // 2
+    HR = M // 2
+    HP = HC // SUB
+    WX_ROWS = 128
+    WX_N = (QW + FF) // WX_ROWS
+    WX_PER = -(-WX_N // ((iters - 1) * GU_N))
     KV_N = M // KV_TOK
 
     me = lax.axis_index("tp")
@@ -64,14 +71,23 @@
 
     def sp_copies(l):
         rem = pl.ds(GU_N * GU_TILE, REM)
-        return [pltpu.make_async_copy(wv.at[l], wsp.at[:, pl.ds(0, HD)], wsp_sem.at[0]),
-                pltpu.make_async_copy(wg.at[l, :, rem], wsp.at[:, pl.ds(HD, REM)], wsp_sem.at[1]),
-                pltpu.make_async_copy(wu.at[l, :, rem], wsp.at[:, pl.ds(HD + REM, REM)], wsp_sem.at[2])]
+        return [pltpu.make_async_copy(wv.at[l], w1.at[1, :, pl.ds(0, HD)], wsp_sem.at[0]),
+                pltpu.make_async_copy(wg.at[l, :, rem], w1.at[1, :, pl.ds(HD, REM)], wsp_sem.at[1]),
+                pltpu.make_async_copy(wu.at[l, :, rem], w1.at[1, :, pl.ds(HD + REM, REM)], wsp_sem.at[2])]
 
     def dn_copies(l, j, slot):
         cols = pl.ds(pl.multiple_of(j * DN_TILE, DN_TILE), DN_TILE)
         return [pltpu.make_async_copy(wo.at[l, :, cols], w2.at[slot, pl.ds(0, QW)], w2_sem.at[slot, 0]),
                 pltpu.make_async_copy(wd.at[l, :, cols], w2.at[slot, pl.ds(QW, FF)], w2_sem.at[slot, 1])]
+
+    def half_cols(core, j):
+        return pl.ds(pl.multiple_of(core * HC + j * SUB, SUB), SUB)
+
+    def dn2_copies(j, slot):
+        own, got = half_cols(low, j), pl.ds(pl.multiple_of(j * SUB, SUB), SUB)
+        return [pltpu.make_async_copy(wo.at[L - 1, :, own], w2.at[slot, pl.ds(0, QW), pl.ds(0, SUB)], w2_sem.at[slot, 0]),
+                pltpu.make_async_copy(wd.at[L - 1, :, own], w2.at[slot, pl.ds(QW, FF), pl.ds(0, SUB)], w2_sem.at[slot, 1]),
+                pltpu.make_async_copy(wx.at[:, got], w2.at[slot, :, pl.ds(SUB, SUB)], w2_sem.at[slot, 2])]
 
     def kv_copies(l, c, b, slot):
         toks = pl.ds(pl.multiple_of(c * M + b * KV_TOK, KV_TOK), KV_TOK)
@@ -105,6 +121,44 @@
             src_ref=share.at[rows_of(peers[k])], dst_ref=recv.at[c, k],
             send_sem=rs_send.at[k], recv_sem=rs_recv.at[c, k, 0],
             device_id={"tp": peers[k]}, device_id_type=MESH)
+
+    def to_sib(src, dst, sems):
+        return pltpu.make_async_remote_copy(
+            src_ref=src, dst_ref=dst, send_sem=sems.at[0], recv_sem=sems.at[1],
+            device_id={"tp": sib}, device_id_type=MESH)
+
+    def wx_send(q):
+        cols = pl.ds(pl.multiple_of((1 - low) * HC, HC), HC)
+        dst = wx.at[pl.ds(pl.multiple_of(q * WX_ROWS, WX_ROWS), WX_ROWS)]
+
+        @pl.when(q * WX_ROWS < QW)
+        def _():
+            to_sib(wo.at[L - 1, pl.ds(pl.multiple_of(q * WX_ROWS, WX_ROWS), WX_ROWS), cols], dst, wx_sem).start()
+
+        @pl.when(jnp.logical_and(q * WX_ROWS >= QW, q < WX_N))
+        def _():
+            to_sib(wd.at[L - 1, pl.ds(pl.multiple_of(q * WX_ROWS - QW, WX_ROWS), WX_ROWS), cols], dst, wx_sem).start()
+
+    def wx_all():
+        return to_sib(wx, wx, wx_sem)
+
+    def hx_copy(start_col, n):
+        cols = pl.ds(pl.multiple_of(start_col, 128), n)
+        return to_sib(hid.at[:, cols], hsib.at[:, cols], hx_sem)
+
+    def hx_all():
+        return to_sib(hid, hsib, hx_sem)
+
+    def xx_copy():
+        cols = pl.ds(pl.multiple_of((1 - low) * HC, HC), HC)
+        return to_sib(xres.at[CHUNKS - 1, :, cols], recv.at[CHUNKS - 1, 2, :, pl.ds(0, HC)], xx_sem)
+
+    def half_share(q, j):
+        return pltpu.make_async_remote_copy(
+            src_ref=share.at[rows_of((1 - half) * 2 + q), half_cols(low, j)],
+            dst_ref=recv.at[CHUNKS - 1, q, :, half_cols(0, j)],
+            send_sem=rs_send.at[q], recv_sem=rs_recv.at[CHUNKS - 1, q, j],
+            device_id={"tp": cross}, device_id_type=MESH)
 
     def gather_copy(c, k):
         block = rows_of(cross) if k == 2 else my_rows
@@ -167,14 +221,17 @@
         for k in range(3):
             gather_copy(c, k).wait_send()
 
-    x_copies = [pltpu.make_async_copy(x_in.at[pl.ds(c * M, M)], act.at[c], io_sem.at[c]) for c in range(CHUNKS)]
+    def x_copy(c):
+        return pltpu.make_async_copy(x_in.at[pl.ds(pl.multiple_of(c * M, M), M)], act.at[c], io_sem.at[c])
+
     res_copies = [pltpu.make_async_copy(x_in.at[pl.ds(pl.multiple_of(c * M + me * Q, Q), Q)], xres.at[c], io_sem.at[CHUNKS + c])
                   for c in range(CHUNKS)]
-    x_copies[0].start()
+    x_copy(0).start()
+    start(sp_copies(0))
     start(qk_copies(0))
-    start(sp_copies(0))
     start(kv_copies(0, 0, 0, 0))
-    start(x_copies[1:])
+    for c in range(1, CHUNKS):
+        x_copy(c).start()
     start(res_copies)
 
     barrier = pltpu.get_barrier_semaphore()
@@ -185,7 +242,7 @@
     grow0 = gain_row(0)
 
     def first_norm(c):
-        x_copies[c].wait()
+        x_copy(c).wait()
 
         def step(r, carry):
             rows = groups_of(r, 0)
@@ -196,7 +253,6 @@
 
         lax.fori_loop(0, M // (ROWS * UNROLL), step, 0)
 
-    first_norm(0)
     wait(res_copies)
 
     lane = lax.broadcasted_iota(jnp.int32, (GRP, 128), 1)
@@ -274,24 +330,42 @@
         nl = (it + 1) // CHUNKS
         nc = (it + 1) % CHUNKS
 
-        @pl.when(it == 1)
-        def _():
-            first_norm(1)
+        @pl.when(it < CHUNKS)
+        def _():
+            first_norm(c)
 
         @pl.when(it >= CHUNKS)
         def _():
             gathered(c)
 
-        start(dn_copies(l, 0, 0))
+        @pl.when(it < iters - 1)
+        def _():
+            start(dn_copies(l, 0, 0))
+
+        @pl.when(it == iters - 1)
+        def _():
+            wx_all().wait_recv()
+            xx_copy().start()
+            start(dn2_copies(0, 0))
+
+        wait(sp_copies(l))
+        r = dot(act[c], w1[1, :, pl.ds(0, HD + 2 * REM)])
+        vnew[...] = r[:, :HD].astype(BF16)
+        hid[:, pl.ds(QW + GU_N * GU_TILE, REM)] = glu(r[:, HD:HD + REM], r[:, HD + REM:])
         wait(qk_copies(l))
         start(gu_copies(l, 0, 1))
         for n in range((QW + HD) // SUB):
             qk[:, pl.ds(n * SUB, SUB)] = dot(act[c], w1[0, :, pl.ds(n * SUB, SUB)]).astype(BF16)
-        wait(sp_copies(l))
-        r = dot(act[c], wsp[...])
-        vnew[...] = r[:, :HD].astype(BF16)
-        hid[:, pl.ds(QW + GU_N * GU_TILE, REM)] = glu(r[:, HD:HD + REM], r[:, HD + REM:])
-        start(dn_copies(l, 1, 1))
+
+        @pl.when(it < iters - 1)
+        def _():
+            start(dn_copies(l, 1, 1))
+
+        @pl.when(it == iters - 1)
+        def _():
+            start(dn2_copies(1, 1))
+            hx_copy(QW + GU_N * GU_TILE, REM).start()
+
 
         def gu_step(j, carry, attend):
             slot = (j + 1) % 2
@@ -309,12 +383,20 @@
             @pl.when(jnp.logical_and(j + 1 == GU_N, it + 1 < iters))
             def _():
                 start(qk_copies(nl))
-                start(sp_copies(nl))
                 start(kv_copies(nl, nc, 0, 0))
 
             @pl.when(jnp.logical_and(j == HOOK_SUM, it > 0))
             def _():
                 sum_and_send(plr, pc)
+
+            @pl.when(it < iters - 1)
+            def _():
+                for i in range(WX_PER):
+                    wx_send((it * GU_N + j) * WX_PER + i)
+
+            @pl.when(jnp.logical_and(it == iters - 1, j > 0))
+            def _():
+                hx_copy(QW + (j - 1) * GU_TILE, GU_TILE).start()
 
             wait(gu_copies(l, j, slot))
             if attend:
@@ -332,13 +414,27 @@
             return carry
 
         lax.fori_loop(0, KV_N, functools.partial(gu_step, attend=True), 0)
+
+        @pl.when(it == iters - 1)
+        def _():
+            hx_copy(0, QW).start()
+
         lax.fori_loop(KV_N, GU_N, functools.partial(gu_step, attend=False), 0)
+
+        @pl.when(it == iters - 1)
+        def _():
+            hx_copy(QW + (GU_N - 1) * GU_TILE, GU_TILE).start()
+
 
         @pl.when(it > 0)
         def _():
             for k in range(3):
                 share_all(pc, k).wait_send()
 
+        @pl.when(it + 1 < iters)
+        def _():
+            start(sp_copies(nl))
+
         def dn_step(j, carry):
             slot = j % 2
 
@@ -347,7 +443,6 @@
                 forward(pc)
 
             wait(dn_copies(l, j, slot))
-
             for n in range(PER):
                 share[:, pl.ds(pl.multiple_of(j * DN_TILE + n * SUB, SUB), SUB)] = dot(
                     hid[...], w2[slot, :, pl.ds(n * SUB, SUB)]).astype(BF16)
@@ -364,8 +459,43 @@
                 send_piece(c, j * PER + n)
             return carry
 
-        lax.fori_loop(0, DN_N, dn_step, 0)
-        send_piece(c, PIECES - 1)
+        def dn2_step(j, carry):
+            slot = j % 2
+
+            @pl.when(j == HOOK_FWD)
+            def _():
+                forward(pc)
+
+            wait(dn2_copies(j, slot))
+            for m in range(0, M, SUB):
+                rows = pl.ds(m, SUB)
+                t = dot(hid[rows, :], w2[slot, :, pl.ds(0, SUB)])
+                if m == 0:
+                    @pl.when(j == 0)
+                    def _():
+                        hx_all().wait_recv()
+                share[rows, half_cols(low, j)] = (t + dot(hsib[rows, :], w2[slot, :, pl.ds(SUB, SUB)])).astype(BF16)
+
+            @pl.when(j + 2 < HP)
+            def _():
+                start(dn2_copies(j + 2, slot))
+
+            @pl.when(j > 0)
+            def _():
+                for q in range(2):
+                    half_share(q, j - 1).start()
+            return carry
+
+        @pl.when(it < iters - 1)
+        def _():
+            lax.fori_loop(0, DN_N, dn_step, 0)
+            send_piece(c, PIECES - 1)
+
+        @pl.when(it == iters - 1)
+        def _():
+            lax.fori_loop(0, HP, dn2_step, 0)
+            for q in range(2):
+                half_share(q, HP - 1).start()
         return carry
 
     lax.fori_loop(0, iters, body, 0)
@@ -373,15 +503,15 @@
     fc = (iters - 1) % CHUNKS
 
     def final_copy(k, j):
-        block = rows_of(cross) if k == 2 else my_rows
+        rows = pl.ds(pl.multiple_of(((1 - half) if k == 2 else half) * HR, HR), HR)
+        ref = act.at[fc, rows, half_cols(low, j)]
         return pltpu.make_async_remote_copy(
-            src_ref=act.at[fc, block, piece(j)], dst_ref=act.at[fc, block, piece(j)],
-            send_sem=fin_send.at[k], recv_sem=fin_recv.at[k, j],
+            src_ref=ref, dst_ref=ref, send_sem=fin_send.at[k], recv_sem=fin_recv.at[k, j],
             device_id={"tp": cross if k == 1 else sib}, device_id_type=MESH)
 
-    def out_copy(j):
-        return pltpu.make_async_copy(
-            act.at[fc, :, piece(j)], out.at[pl.ds(fc * M, M), piece(j)], io_sem.at[fc])
+    def out_copy(j, core):
+        cols = half_cols(core, j)
+        return pltpu.make_async_copy(act.at[fc, :, cols], out.at[pl.ds(fc * M, M), cols], io_sem.at[fc])
 
     out_copies = []
     for c in range(CHUNKS):
@@ -390,43 +520,55 @@
             cp = pltpu.make_async_copy(act.at[c], out.at[pl.ds(c * M, M)], io_sem.at[c])
             cp.start()
             out_copies.append(cp)
+    xx_copy().wait()
 
     def final_sum(j, carry):
-        for k in range(3):
-            share_copy(fc, k, j).wait_recv()
-        for r in range(0, Q, ROWS):
-            own = pl.ds(pl.multiple_of(me * Q + r, ROWS), ROWS)
-            t = share[own, piece(j)].astype(F32)
-            for k in range(3):
-                t = t + recv[fc, k, pl.ds(r, ROWS), piece(j)].astype(F32)
-            act[fc, own, piece(j)] = (xres[fc, pl.ds(r, ROWS), piece(j)].astype(F32) + t).astype(BF16)
+        cols, got = half_cols(low, j), half_cols(0, j)
+        for q in range(2):
+            half_share(q, j).wait_recv()
+            mine = low == q
+            for r in range(0, Q, ROWS):
+                rows = pl.ds(pl.multiple_of((half * 2 + q) * Q + r, ROWS), ROWS)
+                rr = pl.ds(r, ROWS)
+                t = share[rows, cols].astype(F32) + recv[fc, q, rr, got].astype(F32)
+                x = jnp.where(mine, xres[fc, rr, cols].astype(F32), recv[fc, 2, rr, got].astype(F32))
+                act[fc, rows, cols] = (x + t).astype(BF16)
         final_copy(1, j).start()
         final_copy(0, j).start()
         return carry
 
-    lax.fori_loop(0, PIECES, final_sum, 0)
+    lax.fori_loop(0, HP, final_sum, 0)
 
     def final_forward(j, carry):
-        @pl.when(j < PIECES)
+        @pl.when(j < HP)
         def _():
             final_copy(1, j).wait_recv()
             final_copy(2, j).start()
+            out_copy(j, low).start()
 
         @pl.when(j > 0)
         def _():
             final_copy(0, j - 1).wait_recv()
             final_copy(2, j - 1).wait_recv()
-            out_copy(j - 1).start()
+            out_copy(j - 1, 1 - low).start()
         return carry
 
-    lax.fori_loop(0, PIECES + 1, final_forward, 0)
+    lax.fori_loop(0, HP + 1, final_forward, 0)
+
+    own_cols = pl.ds(pl.multiple_of(low * HC, HC), HC)
+    for q in range(2):
+        pltpu.make_async_remote_copy(
+            src_ref=share.at[rows_of((1 - half) * 2 + q), own_cols], dst_ref=recv.at[fc, q, :, pl.ds(0, HC)],
+            send_sem=rs_send.at[q], recv_sem=rs_recv.at[fc, q, 0],
+            device_id={"tp": cross}, device_id_type=MESH).wait_send()
     for k in range(3):
-        share_all(fc, k).wait_send()
-        block = rows_of(cross) if k == 2 else my_rows
+        rows = pl.ds(pl.multiple_of(((1 - half) if k == 2 else half) * HR, HR), HR)
+        ref = act.at[fc, rows, own_cols]
         pltpu.make_async_remote_copy(
-            src_ref=act.at[fc, block], dst_ref=act.at[fc, block], send_sem=fin_send.at[k],
-            recv_sem=fin_recv.at[k, 0], device_id={"tp": cross if k == 1 else sib},
-            device_id_type=MESH).wait_send()
+            src_ref=ref, dst_ref=ref, send_sem=fin_send.at[k], recv_sem=fin_recv.at[k, 0],
+            device_id={"tp": cross if k == 1 else sib}, device_id_type=MESH).wait_send()
+    wx_all().wait_send()
+    hx_all().wait_send()
     pltpu.make_async_copy(act.at[fc], out.at[pl.ds(fc * M, M)], io_sem.at[fc]).wait()
     wait(out_copies)
 
@@ -451,16 +593,14 @@
         vmem = pl.BlockSpec(memory_space=pltpu.VMEM)
         hbm = pl.BlockSpec(memory_space=pl.ANY)
         dma = pltpu.SemaphoreType.DMA
-        rem = ff - (ff // GU_TILE) * GU_TILE
         return pl.pallas_call(
             functools.partial(layers_kernel, tp_size, (L, tok, D, qw, hd, ff, seq)),
-            out_shape=jax.ShapeDtypeStruct((tok, D), BF16),
+            out_shape=[jax.ShapeDtypeStruct((tok, D), BF16), jax.ShapeDtypeStruct((qw + ff, D // 2), BF16)],
             in_specs=[hbm, vmem, vmem, vmem] + [hbm] * 9,
-            out_specs=hbm,
+            out_specs=[hbm, hbm],
             scratch_shapes=[
                 pltpu.VMEM((CHUNKS, M, D), BF16),
                 pltpu.VMEM((2, D, 2 * GU_TILE), BF16),
-                pltpu.VMEM((D, hd + 2 * rem), BF16),
                 pltpu.VMEM((2, qw + ff, DN_TILE), BF16),
                 pltpu.VMEM((M, qw + ff), BF16),
                 pltpu.VMEM((M, qw + hd), BF16),
@@ -473,13 +613,14 @@
                 pltpu.VMEM((KV_TOK // GRP, qw // hd, GRP, hd), F32),
                 pltpu.VMEM((KV_TOK // GRP, qw // hd, GRP, hd), F32),
                 pltpu.VMEM((KV_TOK // GRP, qw // hd * GRP, GRP * seq), BF16),
-                dma((2, 2)), dma((3,)), dma((2, 2)), dma((2, 2)), dma((2 * CHUNKS,)),
+                pltpu.VMEM((M, qw + ff), BF16),
+                dma((2, 2)), dma((3,)), dma((2, 3)), dma((2, 2)), dma((2 * CHUNKS,)),
                 dma((3,)), dma((CHUNKS, 3, D // SUB)), dma((CHUNKS, 3)), dma((CHUNKS, 3)),
-                dma((3,)), dma((3, D // SUB)),
+                dma((3,)), dma((3, D // SUB)), dma((2,)), dma((2,)), dma((2,)),
             ],
             compiler_params=pltpu.CompilerParams(
                 collective_id=0, has_side_effects=True, vmem_limit_bytes=67043328),
             name="layers",
-        )(x_in, lens, cs_t, norm_gain, w_q, w_k, w_v, w_o, w_gate, w_up, w_down, kc, vc)
+        )(x_in, lens, cs_t, norm_gain, w_q, w_k, w_v, w_o, w_gate, w_up, w_down, kc, vc)[0]
 
     return jax.shard_map(per_device, mesh=mesh, in_specs=arg_specs, out_specs=P('dp', None), check_vma=False)

time: 342 us -> 336 us (0.982)
  Pallas kernels: 330 us -> 324 us
    pallas_call x1, Pallas kernels: 330 us -> 324 us  [per_device(): pl.pallas_call(functools.partial(layers_kernel, tp_size, (L, tok, D, qw,...]
where the time goes in v3:
time: 336 us
  Pallas kernels  324 us (96%)
  local copies, waits for them, and re-layouts  8.28 us (2%)
  other arithmetic  3.59 us (1%)
    pallas_call x1, Pallas kernels, per_device(): pl.pallas_call(functools.partial(layers_kernel, tp_size, (L, tok, D, qw,...  324 us

profile of v3, /device:TPU:0, one launch (start us, length us, event | category | flops | bytes accessed | tf_op | source)
XLA Modules:
  0.0 336.0 jit_solution(956696782540539775)
XLA Ops:
  0.0 0.7 convert_element_type.10
  0.7 1.7 broadcast_in_dim.2.refs_1_
  2.4 1.9 multiply_cosine_fusion
  4.3 1.0 pad_maximum_fusion.refs_2_
  5.3 324.2 %layers.1 = (bf16[1024,3584]{1,0:T(8,128)(2,1)}, bf16[5632,1792]{1,0:T(8,128)(2,1)}) custom-call(bf16[1024,3584]{1,0:T(8,128)(2,1)} %refs_0_.1, s32[1024,128]{1,0:T(8,128)} %broadcast_in_dim.2.refs_1_, f32[1024,128]{1,0:T(8,128)} %pad_maximum_fusion.refs_2_, bf16[2,3584]{1,0:T(2,128)(2,1)} %refs_3_.1, bf16[2,3584,896]{2,1,0:T(8,128)(2,1)} %refs_4_.1, ...), custom_call_target="tpu_custom_call" | custom-call | tf_op jit(solution)/shard_map/layers/pallas_call | solution.py:596
  329.4 6.6 %copy.14 = bf16[1024,3584]{1,0:T(8,128)(2,1)} copy(bf16[1024,3584]{1,0:T(8,128)(2,1)} %get-tuple-element.6) | data formatting | bytes 14680064
  (1 shorter events, 0.0 us)

commit v4 on v3

--- a/solution.py
+++ b/solution.py
@@ -21,13 +21,14 @@
 GRP = 16
 ROWS = 16
 UNROLL = 2
+LAG = 3
 HOOK_SUM = 5
 HOOK_FWD = 3
 
 
 def layers_kernel(tp, dims, *refs):
-    (x_in, lens, cs_t, gain, wq, wk, wv, wo, wg, wu, wd, kc, vc, out, wx,
-     act, w1, w2, hid, qk, vnew, kbuf, vbuf, share, recv, xres, logit, selfp, prob, hsib,
+    (x_in, len_in, freq, gain, wq, wk, wv, wo, wg, wu, wd, kc, vc, out, wx,
+     act, w1, w2, hid, qk, vnew, kbuf, vbuf, share, recv, xres, logit, selfp, prob, hsib, lens, cs_t,
      w1_sem, wsp_sem, w2_sem, kv_sem, io_sem, rs_send, rs_recv, ag_send, ag_recv, fin_send, fin_recv,
      wx_sem, hx_sem, xx_sem) = refs
     L, tok, D, QW, HD, FF, SEQ = dims
@@ -45,7 +46,7 @@
     HP = HC // SUB
     WX_ROWS = 128
     WX_N = (QW + FF) // WX_ROWS
-    WX_PER = -(-WX_N // ((iters - 1) * GU_N))
+    WX_PER = -(-WX_N // ((iters - 1) * (GU_N + DN_N)))
     KV_N = M // KV_TOK
 
     me = lax.axis_index("tp")
@@ -253,7 +254,18 @@
 
         lax.fori_loop(0, M // (ROWS * UNROLL), step, 0)
 
-    wait(res_copies)
+
+    def table(i, carry):
+        rows = pl.ds(pl.multiple_of(i * 128, 128), 128)
+        row = len_in[pl.ds(i, 1), :].astype(F32)
+        by_token = jnp.broadcast_to(row, (128, 128)).T
+        ang = by_token * freq[...]
+        lens[rows, :] = by_token.astype(jnp.int32)
+        lanes = lax.broadcasted_iota(jnp.int32, (128, 128), 1)
+        cs_t[rows, :] = jnp.where(lanes < HD // 2, jnp.cos(ang), jnp.sin(ang))
+        return carry
+
+    lax.fori_loop(0, tok // 128, table, 0)
 
     lane = lax.broadcasted_iota(jnp.int32, (GRP, 128), 1)
     trow = lax.broadcasted_iota(jnp.int32, (GRP, 128), 0)
@@ -322,6 +334,30 @@
     def dot(a, b):
         return jnp.dot(a, b, preferred_element_type=F32)
 
+    fc = (iters - 1) % CHUNKS
+
+    def final_copy(k, j):
+        rows = pl.ds(pl.multiple_of(((1 - half) if k == 2 else half) * HR, HR), HR)
+        ref = act.at[fc, rows, half_cols(low, j)]
+        return pltpu.make_async_remote_copy(
+            src_ref=ref, dst_ref=ref, send_sem=fin_send.at[k], recv_sem=fin_recv.at[k, j],
+            device_id={"tp": cross if k == 1 else sib}, device_id_type=MESH)
+
+    def final_sum(j, carry):
+        cols, got = half_cols(low, j), half_cols(0, j)
+        for q in range(2):
+            half_share(q, j).wait_recv()
+            mine = low == q
+            for r in range(0, Q, ROWS):
+                rows = pl.ds(pl.multiple_of((half * 2 + q) * Q + r, ROWS), ROWS)
+                rr = pl.ds(r, ROWS)
+                t = share[rows, cols].astype(F32) + recv[fc, q, rr, got].astype(F32)
+                x = jnp.where(mine, xres[fc, rr, cols].astype(F32), recv[fc, 2, rr, got].astype(F32))
+                act[fc, rows, cols] = (x + t).astype(BF16)
+        final_copy(1, j).start()
+        final_copy(0, j).start()
+        return carry
+
     def body(it, carry):
         l = it // CHUNKS
         c = it % CHUNKS
@@ -333,6 +369,10 @@
         @pl.when(it < CHUNKS)
         def _():
             first_norm(c)
+
+        @pl.when(it == 1)
+        def _():
+            wait(res_copies)
 
         @pl.when(it >= CHUNKS)
         def _():
@@ -392,7 +432,7 @@
             @pl.when(it < iters - 1)
             def _():
                 for i in range(WX_PER):
-                    wx_send((it * GU_N + j) * WX_PER + i)
+                    wx_send((it * (GU_N + DN_N) + j) * WX_PER + i)
 
             @pl.when(jnp.logical_and(it == iters - 1, j > 0))
             def _():
@@ -442,6 +482,9 @@
             def _():
                 forward(pc)
 
+            for i in range(WX_PER):
+                wx_send((it * (GU_N + DN_N) + GU_N + j) * WX_PER + i)
+
             wait(dn_copies(l, j, slot))
             for n in range(PER):
                 share[:, pl.ds(pl.multiple_of(j * DN_TILE + n * SUB, SUB), SUB)] = dot(
@@ -467,8 +510,8 @@
                 forward(pc)
 
             wait(dn2_copies(j, slot))
-            for m in range(0, M, SUB):
-                rows = pl.ds(m, SUB)
+            for m in range(2):
+                rows = pl.ds(pl.multiple_of((1 - half if m == 0 else half) * HR, HR), HR)
                 t = dot(hid[rows, :], w2[slot, :, pl.ds(0, SUB)])
                 if m == 0:
                     @pl.when(j == 0)
@@ -480,10 +523,16 @@
             def _():
                 start(dn2_copies(j + 2, slot))
 
-            @pl.when(j > 0)
-            def _():
-                for q in range(2):
-                    half_share(q, j - 1).start()
+            for q in range(2):
+                half_share(q, j).start()
+
+            @pl.when(j == LAG)
+            def _():
+                xx_copy().wait()
+
+            @pl.when(j >= LAG)
+            def _():
+                final_sum(j - LAG, 0)
             return carry
 
         @pl.when(it < iters - 1)
@@ -494,20 +543,9 @@
         @pl.when(it == iters - 1)
         def _():
             lax.fori_loop(0, HP, dn2_step, 0)
-            for q in range(2):
-                half_share(q, HP - 1).start()
         return carry
 
     lax.fori_loop(0, iters, body, 0)
-
-    fc = (iters - 1) % CHUNKS
-
-    def final_copy(k, j):
-        rows = pl.ds(pl.multiple_of(((1 - half) if k == 2 else half) * HR, HR), HR)
-        ref = act.at[fc, rows, half_cols(low, j)]
-        return pltpu.make_async_remote_copy(
-            src_ref=ref, dst_ref=ref, send_sem=fin_send.at[k], recv_sem=fin_recv.at[k, j],
-            device_id={"tp": cross if k == 1 else sib}, device_id_type=MESH)
 
     def out_copy(j, core):
         cols = half_cols(core, j)
@@ -520,24 +558,8 @@
             cp = pltpu.make_async_copy(act.at[c], out.at[pl.ds(c * M, M)], io_sem.at[c])
             cp.start()
             out_copies.append(cp)
-    xx_copy().wait()
-
-    def final_sum(j, carry):
-        cols, got = half_cols(low, j), half_cols(0, j)
-        for q in range(2):
-            half_share(q, j).wait_recv()
-            mine = low == q
-            for r in range(0, Q, ROWS):
-                rows = pl.ds(pl.multiple_of((half * 2 + q) * Q + r, ROWS), ROWS)
-                rr = pl.ds(r, ROWS)
-                t = share[rows, cols].astype(F32) + recv[fc, q, rr, got].astype(F32)
-                x = jnp.where(mine, xres[fc, rr, cols].astype(F32), recv[fc, 2, rr, got].astype(F32))
-                act[fc, rows, cols] = (x + t).astype(BF16)
-        final_copy(1, j).start()
-        final_copy(0, j).start()
-        return carry
-
-    lax.fori_loop(0, HP, final_sum, 0)
+
+    lax.fori_loop(HP - LAG, HP, final_sum, 0)
 
     def final_forward(j, carry):
         @pl.when(j < HP)
@@ -583,9 +605,8 @@
         qw = w_q.shape[2]
         ff = w_gate.shape[2]
         inv_freq = 1.0 / (ROPE_BASE ** (jnp.arange(0, hd, 2).astype(F32) / hd))
-        ang = lengths.astype(F32)[:, None] * inv_freq[None, :]
-        cs_t = jnp.concatenate([jnp.cos(ang), jnp.sin(ang)], axis=-1)
-        lens = jnp.broadcast_to(lengths[:, None], (tok, 128))
+        freq = jnp.concatenate([inv_freq, inv_freq])[None, :]
+        len_in = lengths.reshape(tok // 128, 128)
         kc = k_cache.reshape(L, tok, seq, hd)
         vc = v_cache.reshape(L, tok, seq, hd)
         M = tok // CHUNKS
@@ -614,6 +635,8 @@
                 pltpu.VMEM((KV_TOK // GRP, qw // hd, GRP, hd), F32),
                 pltpu.VMEM((KV_TOK // GRP, qw // hd * GRP, GRP * seq), BF16),
                 pltpu.VMEM((M, qw + ff), BF16),
+                pltpu.VMEM((tok, 128), jnp.int32),
+                pltpu.VMEM((tok, 128), F32),
                 dma((2, 2)), dma((3,)), dma((2, 3)), dma((2, 2)), dma((2 * CHUNKS,)),
                 dma((3,)), dma((CHUNKS, 3, D // SUB)), dma((CHUNKS, 3)), dma((CHUNKS, 3)),
                 dma((3,)), dma((3, D // SUB)), dma((2,)), dma((2,)), dma((2,)),
@@ -621,6 +644,6 @@
             compiler_params=pltpu.CompilerParams(
                 collective_id=0, has_side_effects=True, vmem_limit_bytes=67043328),
             name="layers",
-        )(x_in, lens, cs_t, norm_gain, w_q, w_k, w_v, w_o, w_gate, w_up, w_down, kc, vc)[0]
+        )(x_in, len_in, freq, norm_gain, w_q, w_k, w_v, w_o, w_gate, w_up, w_down, kc, vc)[0]
 
     return jax.shard_map(per_device, mesh=mesh, in_specs=arg_specs, out_specs=P('dp', None), check_vma=False)

time: 336 us -> 322 us (0.958)
  Pallas kernels: 324 us -> 314 us
    pallas_call x1, Pallas kernels: 324 us -> 314 us  [per_device(): pl.pallas_call(functools.partial(layers_kernel, tp_size, (L, tok, D, qw,...]
where the time goes in v4:
time: 322 us; the launch traced here: 321 us
  Pallas kernels  314 us (98%)
  local copies, waits for them, and re-layouts  6.6 us (2%)
    pallas_call x1, Pallas kernels, per_device(): pl.pallas_call(functools.partial(layers_kernel, tp_size, (L, tok, D, qw,...  314 us
    unnamed x1, local copies, waits for them, and re-layouts  6.6 us

profile of v4, /device:TPU:0, one launch (start us, length us, event | category | flops | bytes accessed | tf_op | source)
XLA Modules:
  0.0 321.2 jit_solution(6992720249577348903)
XLA Ops:
  0.0 0.6 maximum_bitcast_fusion.refs_2_
  0.6 314.0 %layers.1 = (bf16[1024,3584]{1,0:T(8,128)(2,1)}, bf16[5632,1792]{1,0:T(8,128)(2,1)}) custom-call(bf16[1024,3584]{1,0:T(8,128)(2,1)} %refs_0_.1, s32[8,128]{1,0:T(8,128)} %bitcast.7, f32[1,128]{1,0:T(1,128)} %maximum_bitcast_fusion.refs_2_, bf16[2,3584]{1,0:T(2,128)(2,1)} %refs_3_.1, bf16[2,3584,896]{2,1,0:T(8,128)(2,1)} %refs_4_.1, ...), custom_call_target="tpu_custom_call" | custom-call | tf_op jit(solution)/shard_map/layers/pallas_call | solution.py:617
  314.6 6.6 %copy.14 = bf16[1024,3584]{1,0:T(8,128)(2,1)} copy(bf16[1024,3584]{1,0:T(8,128)(2,1)} %get-tuple-element.6) | data formatting | bytes 14680064
  (1 shorter events, 0.0 us)
